TPU v7x, 256 devices: a whole 4x4x8 slice. The times are simulated.
256 devices in a mesh: dp: 2 (over y_hi), tm: 32 (over z, y_lo, core), rows: 4 (over x).
Axes of the slice: x: 4, y: 4 (y_hi: 2, y_lo: 2; y = y_hi * 2 + y_lo), z: 8, core: 2. Of those that a mesh axis runs over, the one named last changes fastest.
Arguments:
- clips: bfloat16 [2, 64, 4, 128, 256], P('dp', 'tm', 'rows'), may hold values from -12 to 12
- weight: bfloat16 [3, 3, 3, 256, 256], replicated, may hold values from -0.078125 to 0.078125
- bias: float32 [256], replicated, may hold values from -1 to 1
- head: float32 [256], replicated, may hold values from -4 to 4
Outputs:
- grad_weight: float32 [3, 3, 3, 256, 256], replicated
- grad_bias: float32 [256], replicated
- grad_head: float32 [256], replicated
All inputs are finite; a program needn't handle non-finite values.
Results may differ from a plain program's by a relative error of at most 0.0003.
Values may be sent and summed in bfloat16 or wider, within the bound.
A program may use at most 128 MiB of HBM per device.

v0:
```python
import functools
import math

import jax
import jax.numpy as jnp
from jax import lax
from jax.experimental import pallas as pl
from jax.experimental.pallas import tpu as pltpu
from jax.sharding import PartitionSpec as P

penalty_weight = 0.01
MESH = pl.DeviceIdType.MESH
SUB = 8
TAPS = 3
SPAN = 120.0


def make_plan(sizes, shares):
    dp, tm, rows = sizes
    cuts, rest, left = [], [], shares
    near = 2 if rows % 2 == 0 else 1
    for axis, stride, count in (("rows", 1, near), ("rows", near, rows // near), ("dp", 1, dp), ("tm", 1, tm)):
        cut = 1
        while count % (2 * cut) == 0 and left % (2 * cut) == 0:
            cut *= 2
        left //= cut
        cuts.append((axis, stride, cut))
        rest.append((axis, stride * cut, count // cut))
    pair, far, depth, line = cuts
    rest = tuple(group for group in rest if group[2] > 1)
    across, along, ahead = (far, depth, line), (depth, far, line), (line, depth, far)
    between = (depth, line, far)
    return pair, (ahead, along, across, between, across, along), rest


def kernel(
    sizes, plan, clips_ref, weight_ref, bias_ref, head_ref,
    out_ref, bias_out, head_out,
    w_ref, clip_pad, score_pad, grad_pad, acc, slope_ref, curve_ref, cat_s, cat_p, total,
    land_pair, code, land, full, small_mine, small_land,
    local_sem, halo_send, halo_recv, pair_send, pair_recv, part_send, part_recv, gath_send, gath_recv,
    small_send, small_recv, out_sem,
):
    small_refs = (bias_out, head_out)
    dp, tm, rows = sizes
    frames, cols, chans = clips_ref.shape
    count = frames * cols
    me = {"dp": lax.axis_index("dp"), "tm": lax.axis_index("tm"), "rows": lax.axis_index("rows")}

    def device(**moved):
        place = dict(me, **moved)
        return (place["dp"], place["tm"], place["rows"])

    weight_copy = pltpu.make_async_copy(weight_ref, w_ref, local_sem.at[0])
    weight_copy.start()
    clip_copy = pltpu.make_async_copy(
        clips_ref, clip_pad.at[pl.ds(1, frames), 1], local_sem.at[1]
    )
    clip_copy.start()
    for pad in (clip_pad, score_pad, grad_pad):
        pad[:, 0] = jnp.zeros((frames + 2, cols, chans), pad.dtype)
        pad[:, 2] = jnp.zeros((frames + 2, cols, chans), pad.dtype)
        pad[0, 1] = jnp.zeros((cols, chans), pad.dtype)
        pad[frames + 1, 1] = jnp.zeros((cols, chans), pad.dtype)

    barrier = pltpu.get_barrier_semaphore()
    flat = me["tm"] * rows + me["rows"]
    plane = tm * rows

    def greet(step, carry):
        other = lax.rem(flat + step, plane)
        pl.semaphore_signal(
            barrier, inc=1, device_id=device(tm=other // rows, rows=lax.rem(other, rows)),
            device_id_type=MESH,
        )
        return carry

    lax.fori_loop(1, plane, greet, 0)
    for step in range(1, dp):
        pl.semaphore_signal(
            barrier, inc=1, device_id=device(dp=lax.rem(me["dp"] + step, dp)), device_id_type=MESH
        )
    pl.semaphore_wait(barrier, plane - 1 + dp - 1)

    moves = [(t, r) for t in (-1, 0, 1) for r in (-1, 0, 1) if (t, r) != (0, 0)]

    def inside(t, r):
        ok = None
        for axis, step, size in (("tm", t, tm), ("rows", r, rows)):
            if step:
                cond = me[axis] > 0 if step < 0 else me[axis] < size - 1
                ok = cond if ok is None else jnp.logical_and(ok, cond)
        return ok

    def halo_copy(which, pad, source, t, r):
        slot = which * len(moves) + moves.index((t, r))
        if t == 0:
            here, there = pl.ds(0, frames), pl.ds(1, frames)
        elif t > 0:
            here, there = pl.ds(frames - 1, 1), pl.ds(0, 1)
        else:
            here, there = pl.ds(0, 1), pl.ds(frames + 1, 1)
        return pltpu.make_async_remote_copy(
            src_ref=source.at[here], dst_ref=pad.at[there, 1 - r],
            send_sem=halo_send.at[slot], recv_sem=halo_recv.at[slot],
            device_id=device(tm=me["tm"] + t, rows=me["rows"] + r), device_id_type=MESH,
        )

    def halo_start(which, pad, source):
        for t, r in moves:
            @pl.when(inside(t, r))
            def _():
                halo_copy(which, pad, source, t, r).start()

    def halo_wait(which, pad, source, level):
        for t, r in moves:
            if (t == 0) != level:
                continue

            @pl.when(inside(t, r))
            def _():
                halo_copy(which, pad, source, t, r).wait_send()

            @pl.when(inside(-t, -r))
            def _():
                halo_copy(which, pad, source, t, r).wait_recv()

    column = lax.rem(lax.broadcasted_iota(jnp.int32, (count, chans), 0), cols)

    def earlier(value):
        return jnp.where(column == 0, 0.0, pltpu.roll(value, 1, 0))

    def later(value):
        return jnp.where(column == cols - 1, 0.0, pltpu.roll(value, count - 1, 0))

    def conv(which, pad, source, transpose):
        def step(a):
            base = (TAPS - 1 - a) if transpose else a
            pieces = [
                pad[pl.ds(base, frames), (TAPS - 1 - b) if transpose else b].reshape(count, chans)
                for b in range(TAPS)
            ]
            left = jnp.concatenate(pieces, axis=1)
            for d in range(TAPS):
                taps = [w_ref[(a * TAPS + b) * TAPS + d] for b in range(TAPS)]
                if transpose:
                    part = lax.dot_general(
                        left, jnp.concatenate(taps, axis=1), (((1,), (1,)), ((), ())),
                        preferred_element_type=jnp.float32,
                    )
                else:
                    part = jnp.dot(
                        left, jnp.concatenate(taps, axis=0), preferred_element_type=jnp.float32
                    )
                acc[d] = part if a == 1 else acc[d] + part

        halo_wait(which, pad, source, True)
        step(1)
        halo_wait(which, pad, source, False)
        step(0)
        step(2)
        if transpose:
            return later(acc[0]) + acc[1] + earlier(acc[2])
        return earlier(acc[0]) + acc[1] + later(acc[2])

    def shifted(value):
        value = value.astype(jnp.float32)
        return jnp.concatenate(
            [later(value), value, earlier(value)], axis=1
        ).astype(jnp.bfloat16)

    halo_start(0, clip_pad, clips_ref)
    clip_copy.wait()
    weight_copy.wait()
    pre = conv(0, clip_pad, clips_ref, False) + bias_ref[...]
    sig = jax.nn.sigmoid(pre)
    slope = sig * (1.0 + pre * (1.0 - sig))
    slope_ref[...] = slope
    curve_ref[...] = sig * (1.0 - sig) * (2.0 + pre * (1.0 - 2.0 * sig))
    score = (head_ref[...] * slope).astype(jnp.bfloat16)
    score_pad[pl.ds(1, frames), 1] = score.reshape(frames, cols, chans)
    score_own = score_pad.at[pl.ds(1, frames), 1]
    cat_s[...] = shifted(score)
    halo_start(1, score_pad, score_own)

    input_grad = conv(1, score_pad, score_own, True).astype(jnp.bfloat16)
    grad_pad[pl.ds(1, frames), 1] = input_grad.reshape(frames, cols, chans)
    grad_own = grad_pad.at[pl.ds(1, frames), 1]
    halo_start(2, grad_pad, grad_own)

    back = penalty_weight * conv(2, grad_pad, grad_own, False)
    pre_grad = back * head_ref[...] * curve_ref[...]
    cat_p[...] = shifted(pre_grad.astype(jnp.bfloat16))
    small_mine[...] = jnp.zeros_like(small_mine)
    small_mine[pl.ds(0, 1)] = jnp.sum(pre_grad, axis=0, keepdims=True)
    small_mine[pl.ds(1, 1)] = jnp.sum(back * slope_ref[...], axis=0, keepdims=True)

    pair, orders, rest = plan
    parts, shares, taps = total.shape[:3]
    lanes = land.shape[-1]
    split = chans // lanes
    half = shares // pair[2]
    units = chans // SUB

    def place_in(group):
        axis, stride, size = group
        return lax.rem(me[axis] // stride, size)

    def peer(group, step):
        axis, stride, size = group
        mine = place_in(group)
        other = lax.rem(mine + step, size)
        return other, device(**{axis: me[axis] + (other - mine) * stride})

    def pair_copy(a):
        other, target = peer(pair, 1)
        here = pl.ds(a * split, split)
        return pltpu.make_async_remote_copy(
            src_ref=total.at[here, pl.ds(other * half, half)], dst_ref=land_pair.at[here],
            send_sem=pair_send.at[a], recv_sem=pair_recv.at[a],
            device_id=target, device_id_type=MESH,
        )

    def correlate(a):
        def step(b, carry):
            dims = (((0,), (0,)), ((), ()))
            first = lax.dot_general(
                grad_pad[a : a + frames, b].reshape(count, chans), cat_s[...], dims,
                preferred_element_type=jnp.float32,
            )
            second = lax.dot_general(
                clip_pad[a : a + frames, b].reshape(count, chans), cat_p[...], dims,
                preferred_element_type=jnp.float32,
            )
            both = penalty_weight * first + second
            for d in range(TAPS):
                for p in range(split):
                    at = d * chans + p * lanes
                    total[a * split + p, :, b * TAPS + d] = both[:, at : at + lanes].reshape(
                        units, SUB, lanes
                    )
            return carry

        lax.fori_loop(0, TAPS, step, 0)
        if pair[2] > 1:
            pair_copy(a).start()

    def finish_pair(a):
        if pair[2] == 1:
            return
        mine = place_in(pair) * half
        pair_copy(a).wait()

        def add(step, carry):
            for p in range(a * split, (a + 1) * split):
                total[p, mine + step] = total[p, mine + step] + land_pair[p, step]
            return carry

        lax.fori_loop(0, half, add, 0)

    def encode(value):
        top = (jnp.max(jnp.abs(value), axis=0) * 1.01 + 1e-30).astype(jnp.bfloat16)
        rate = SPAN / top.astype(jnp.float32)
        return jnp.exp2(value * rate[None]).astype(jnp.bfloat16), top

    sems = {"part": 0, "gath": 0, "land": 0}

    def scatter_start(p, group, base, size, whole=False):
        share = size if whole else size // group[2]
        copies = []
        for step in range(1, group[2]):
            other, target = peer(group, step)
            origin = base if whole else base + other * share
            at = sems["land"]

            def fill(k, carry):
                value, top = encode(total[p, origin + k])
                code[at + k, pl.ds(0, taps)] = value
                code[at + k, taps] = top
                return carry

            lax.fori_loop(0, share, fill, 0)
            copy = pltpu.make_async_remote_copy(
                src_ref=code.at[pl.ds(at, share)], dst_ref=land.at[pl.ds(at, share)],
                send_sem=part_send.at[sems["part"]], recv_sem=part_recv.at[sems["part"]],
                device_id=target, device_id_type=MESH,
            )
            copy.start()
            copies.append((copy, at))
            sems["land"] += share
            sems["part"] += 1
        return copies, base if whole else base + place_in(group) * share, share

    def scatter_end(p, copies, base, share):
        for copy, _ in copies:
            copy.wait()
        if not copies:
            return

        def add(step, carry):
            value = total[p, base + step]
            for _, at in copies:
                value = value + decode(land[at + step], taps)
            total[p, base + step] = value
            return carry

        lax.fori_loop(0, share, add, 0)

    def gather_start(p, group, base, size):
        copies = []
        for step in range(1, group[2]):
            _, target = peer(group, step)
            block = full.at[p, pl.ds(base, size)]
            copy = pltpu.make_async_remote_copy(
                src_ref=block, dst_ref=block,
                send_sem=gath_send.at[sems["gath"]], recv_sem=gath_recv.at[sems["gath"]],
                device_id=target, device_id_type=MESH,
            )
            copy.start()
            copies.append(copy)
            sems["gath"] += 1
        return copies

    base = place_in(pair) * half
    state = [(base, half)] * parts
    trail = [[] for _ in range(parts)]
    started = [None] * parts
    depth = len(orders[0])

    def small_start(number, group, at):
        copies = []
        for step in range(1, group[2]):
            _, target = peer(group, step)
            copy = pltpu.make_async_remote_copy(
                src_ref=small_mine.at[pl.ds(number * SUB, SUB)],
                dst_ref=small_land.at[pl.ds(at * SUB, SUB)],
                send_sem=small_send.at[at], recv_sem=small_recv.at[at],
                device_id=target, device_id_type=MESH,
            )
            copy.start()
            copies.append((copy, at))
            at += 1
        return copies

    def small_end(number, copies):
        value = small_mine[pl.ds(number * SUB, SUB)]
        for copy, _ in copies:
            copy.wait()
        for _, slot in copies:
            value = value + small_land[pl.ds(slot * SUB, SUB)]
        small_mine[pl.ds((number + 1) * SUB, SUB)] = value

    def scatter(p, level):
        if level < depth:
            trail[p].append(state[p])
            started[p] = scatter_start(p, orders[p][level], *state[p])
        else:
            started[p] = scatter_start(p, rest[level - depth], *state[p], True)

    def end_scatter(p):
        copies, base, share = started[p]
        scatter_end(p, copies, base, share)
        state[p] = (base, share)

    small_groups = (pair, *orders[0], *rest)
    small_at = 0
    for a in range(TAPS):
        correlate(a)
        if a == 0:
            small = small_start(0, small_groups[0], small_at)
            small_at += len(small)
        else:
            finish_pair(a - 1)
            for p in range((a - 1) * split, a * split):
                scatter(p, 0)
    small_end(0, small)
    finish_pair(TAPS - 1)
    for p in range(parts - split, parts):
        scatter(p, 0)
    levels = depth + len(rest)
    for level in range(1, levels + 1):
        small = small_start(level, small_groups[level], small_at)
        small_at += len(small)
        for p in range(parts):
            end_scatter(p)
            if level < levels:
                scatter(p, level)
                continue
            base, size = state[p]

            def keep(k, carry):
                value, top = encode(total[p, base + k])
                full[p, base + k, pl.ds(0, taps)] = value
                full[p, base + k, taps] = top
                return carry

            lax.fori_loop(0, size, keep, 0)
            started[p] = gather_start(p, orders[p][depth - 1], *state[p])
        small_end(level, small)
    for k in range(2):
        small_refs[k][...] = small_mine[pl.ds((levels + 1) * SUB + k, 1)]
    for level in reversed(range(depth)):
        for p in range(parts):
            for copy in started[p]:
                copy.wait()
            state[p] = trail[p][level]
            group = orders[p][level - 1] if level else pair
            started[p] = gather_start(p, group, *state[p])
    outs = []
    for p in range(parts):
        for copy in started[p]:
            copy.wait()
        copy = pltpu.make_async_copy(full.at[p], out_ref.at[p], out_sem.at[p])
        copy.start()
        outs.append(copy)
    for copy in outs:
        copy.wait()


def decode(block, taps):
    unit = block[taps].astype(jnp.float32) * (1.0 / (SPAN * math.log(2.0)))
    return jnp.log(block[:taps].astype(jnp.float32)) * unit[None]


def decode_kernel(code_ref, bias_ref, head_ref, out_ref, bias_out, head_out):
    parts, shares, blocks, _, lanes = code_ref.shape
    taps = blocks - 1
    split = parts // TAPS
    for p in range(parts):
        at, lane = p // split * taps, p % split * lanes
        for k in range(shares):
            out_ref[at : at + taps, k, :, lane : lane + lanes] = decode(code_ref[p, k], taps)
    bias_out[...] = bias_ref[...]
    head_out[...] = head_ref[...]


def per_device(sizes, clips, weight, bias, head):
    _, frames, _, cols, chans = clips.shape
    count = frames * cols
    split = 2
    taps, shares, parts = TAPS**2, chans // SUB, TAPS * split
    lanes = chans // split
    plan = make_plan(sizes, shares)
    pair, orders, rest = plan
    half = shares // pair[2]
    small_n = sum(g[2] - 1 for g in (pair,) + orders[0] + rest)
    land = parts_n = gath_n = 0
    for order in orders:
        size = half
        for group in order:
            land += size // group[2] * (group[2] - 1)
            size //= group[2]
            parts_n += group[2] - 1
        for group in rest:
            land += size * (group[2] - 1)
            parts_n += group[2] - 1
        gath_n += sum(g[2] - 1 for g in order) + pair[2] - 1
    pad = pltpu.VMEM((frames + 2, 3, cols, chans), jnp.bfloat16)
    field = pltpu.VMEM((count, chans), jnp.float32)
    coded = pltpu.VMEM((max(land, 1), taps + 1, SUB, lanes), jnp.bfloat16)
    dma = pltpu.SemaphoreType.DMA
    vmem = pl.BlockSpec(memory_space=pltpu.VMEM)
    hbm = pl.BlockSpec(memory_space=pl.ANY)
    row = jax.ShapeDtypeStruct((1, chans), jnp.float32)
    code, *small = pl.pallas_call(
        functools.partial(kernel, sizes, plan),
        out_shape=(
            jax.ShapeDtypeStruct((parts, shares, taps + 1, SUB, lanes), jnp.bfloat16),
            row, row,
        ),
        in_specs=[hbm, hbm, vmem, vmem],
        out_specs=(hbm, vmem, vmem),
        scratch_shapes=[
            pltpu.VMEM((TAPS**3, chans, chans), jnp.bfloat16),
            pad, pad, pad,
            pltpu.VMEM((TAPS, count, chans), jnp.float32),
            field, field,
            pltpu.VMEM((count, TAPS * chans), jnp.bfloat16),
            pltpu.VMEM((count, TAPS * chans), jnp.bfloat16),
            pltpu.VMEM((parts, shares, taps, SUB, lanes), jnp.float32),
            pltpu.VMEM((parts, half, taps, SUB, lanes), jnp.float32),
            coded, coded,
            pltpu.VMEM((parts, shares, taps + 1, SUB, lanes), jnp.bfloat16),
            pltpu.VMEM(((len(rest) + 6) * SUB, chans), jnp.float32),
            pltpu.VMEM((max(small_n, 1) * SUB, chans), jnp.float32),
            dma((2,)), dma((24,)), dma((24,)), dma((TAPS,)), dma((TAPS,)),
            dma((max(parts_n, 1),)), dma((max(parts_n, 1),)),
            dma((max(gath_n, 1),)), dma((max(gath_n, 1),)),
            dma((max(small_n, 1),)), dma((max(small_n, 1),)), dma((parts,)),
        ],
        compiler_params=pltpu.CompilerParams(
            collective_id=0, has_side_effects=True, vmem_limit_bytes=60 * 1024 * 1024
        ),
    )(
        clips.reshape(frames, cols, chans),
        weight.reshape(TAPS**3, chans, chans),
        bias.reshape(1, chans),
        head.reshape(1, chans),
    )
    step = math.gcd(shares, 8)
    short = pl.BlockSpec((1, chans), lambda i: (0, 0))
    grad_weight, grad_bias, grad_head = pl.pallas_call(
        decode_kernel,
        out_shape=(jax.ShapeDtypeStruct((TAPS**3, shares, SUB, chans), jnp.float32), row, row),
        grid=(shares // step,),
        in_specs=[
            pl.BlockSpec((parts, step, taps + 1, SUB, lanes), lambda i: (0, i, 0, 0, 0)),
            short, short,
        ],
        out_specs=(
            pl.BlockSpec((TAPS**3, step, SUB, chans), lambda i: (0, i, 0, 0)), short, short
        ),
    )(code, *small)
    grad_weight = grad_weight.reshape(TAPS, TAPS, TAPS, chans, chans)
    return grad_weight, grad_bias.reshape(chans), grad_head.reshape(chans)


def solution(mesh):
    sizes = tuple(mesh.shape[axis] for axis in ("dp", "tm", "rows"))
    return jax.shard_map(
        functools.partial(per_device, sizes),
        mesh=mesh,
        in_specs=(P("dp", "tm", "rows", None, None), P(), P(), P()),
        out_specs=(P(), P(), P()),
        check_vma=False,
    )
```

profile of v0, /device:TPU:1, one launch (start us, length us, event | category | flops | bytes accessed | tf_op | source)
XLA Modules:
  0.0 222.7 jit_solution(14969546048174457061)
XLA Ops:
  0.6 216.3 %shard_map.67 = (bf16[6,32,10,8,128]{4,3,2,1,0:T(8,128)(2,1)}, f32[1,256]{1,0:T(1,128)}, f32[1,256]{1,0:T(1,128)}) custom-call(bf16[2,128,256]{2,1,0:T(8,128)(2,1)} %bitcast.8, bf16[27,256,256]{2,1,0:T(8,128)(2,1)} %bitcast.7, f32[1,256]{1,0:T(1,128)} %bitcast.9, f32[1,256]{1,0:T(1,128)} %bitcast.10), custom_call_target="tpu_custom_call" | custom-call | tf_op jit(solution)/shard_map/pallas_call | solution.py:465
  216.9 5.8 %shard_map.68 = (f32[27,32,8,256]{3,2,1,0:T(8,128)}, f32[1,256]{1,0:T(1,128)}, f32[1,256]{1,0:T(1,128)}) custom-call(bf16[6,32,10,8,128]{4,3,2,1,0:T(8,128)(2,1)} %get-tuple-element.9.code_ref, f32[1,256]{1,0:T(1,128)} %get-tuple-element.10.bias_ref, f32[1,256]{1,0:T(1,128)} %get-tuple-element.11.head_ref), custom_call_target="tpu_custom_call" | custom-call | tf_op jit(solution)/shard_map/pallas_call | solution.py:502
where the time goes:
time: 223 us
  Pallas kernels  222 us (100%)
    pallas_call x1, Pallas kernels, per_device(): pl.pallas_call(functools.partial(kernel, sizes, plan), out_shape=(jax.Sha...  216 us
    pallas_call x1, Pallas kernels, per_device(): pl.pallas_call(decode_kernel, out_shape=(jax.ShapeDtypeStruct((TAPS ** 3,...  5.79 us

commit v1 on v0

--- a/solution.py
+++ b/solution.py
@@ -17,20 +17,11 @@
 
 def make_plan(sizes, shares):
     dp, tm, rows = sizes
-    cuts, rest, left = [], [], shares
-    near = 2 if rows % 2 == 0 else 1
-    for axis, stride, count in (("rows", 1, near), ("rows", near, rows // near), ("dp", 1, dp), ("tm", 1, tm)):
-        cut = 1
-        while count % (2 * cut) == 0 and left % (2 * cut) == 0:
-            cut *= 2
-        left //= cut
-        cuts.append((axis, stride, cut))
-        rest.append((axis, stride * cut, count // cut))
-    pair, far, depth, line = cuts
-    rest = tuple(group for group in rest if group[2] > 1)
-    across, along, ahead = (far, depth, line), (depth, far, line), (line, depth, far)
-    between = (depth, line, far)
-    return pair, (ahead, along, across, between, across, along), rest
+    pair = ("tm", 1, 2)
+    wide, near, deep = ("rows", 1, rows), ("tm", 2, 2), ("dp", 1, dp)
+    rest = (("tm", 4, tm // 4),)
+    across, along, ahead = (wide, near, deep), (near, deep, wide), (deep, near, wide)
+    return pair, (across, along, across, ahead, across, along), rest
 
 
 def kernel(

time: 223 us -> 124 us (0.56)
  Pallas kernels: 222 us -> 123 us
    pallas_call x1, Pallas kernels: 216 us -> 117 us  [per_device(): pl.pallas_call(functools.partial(kernel, sizes, plan), out_shape=(jax.Sha...]
where the time goes in v1:
time: 124 us; the launch traced here: 123 us
  Pallas kernels  123 us (99%)
    pallas_call x1, Pallas kernels, per_device(): pl.pallas_call(functools.partial(kernel, sizes, plan), out_shape=(jax.Sha...  117 us
    pallas_call x1, Pallas kernels, per_device(): pl.pallas_call(decode_kernel, out_shape=(jax.ShapeDtypeStruct((TAPS ** 3,...  5.79 us

profile of v1, /device:TPU:1, one launch (start us, length us, event | category | flops | bytes accessed | tf_op | source)
XLA Modules:
  0.0 123.3 jit_solution(9231047429996462241)
XLA Ops:
  0.6 116.9 %shard_map.67 = (bf16[6,32,10,8,128]{4,3,2,1,0:T(8,128)(2,1)}, f32[1,256]{1,0:T(1,128)}, f32[1,256]{1,0:T(1,128)}) custom-call(bf16[2,128,256]{2,1,0:T(8,128)(2,1)} %bitcast.8, bf16[27,256,256]{2,1,0:T(8,128)(2,1)} %bitcast.7, f32[1,256]{1,0:T(1,128)} %bitcast.9, f32[1,256]{1,0:T(1,128)} %bitcast.10), custom_call_target="tpu_custom_call" | custom-call | tf_op jit(solution)/shard_map/pallas_call | solution.py:456
  117.5 5.8 %shard_map.68 = (f32[27,32,8,256]{3,2,1,0:T(8,128)}, f32[1,256]{1,0:T(1,128)}, f32[1,256]{1,0:T(1,128)}) custom-call(bf16[6,32,10,8,128]{4,3,2,1,0:T(8,128)(2,1)} %get-tuple-element.9.code_ref, f32[1,256]{1,0:T(1,128)} %get-tuple-element.10.bias_ref, f32[1,256]{1,0:T(1,128)} %get-tuple-element.11.head_ref), custom_call_target="tpu_custom_call" | custom-call | tf_op jit(solution)/shard_map/pallas_call | solution.py:493

commit v2 on v1

v2 whole, which is shorter than its diff:
```python
import functools
import math

import jax
import jax.numpy as jnp
from jax import lax
from jax.experimental import pallas as pl
from jax.experimental.pallas import tpu as pltpu
from jax.sharding import PartitionSpec as P

penalty_weight = 0.01
MESH = pl.DeviceIdType.MESH
SUB = 8
LANES = 128
TAPS = 3
SPAN = 120.0
RING = 4
DEEP = 8
CORES = 2
GROUPS = 4
SHARE = 7
UNITS = 16
PARTS = 2 * GROUPS


def flip(m):
    return m + 1 - 2 * lax.rem(m, 2)


def mirror(m):
    return RING - 1 - m


def kernel(
    sizes, clips_ref, weight_ref, bias_ref, head_ref,
    out_ref, bias_out, head_out,
    w_ref, clip_pad, score_pad, grad_pad, acc, slope_ref, curve_ref,
    cat_s, cat_p, stage_s, stage_p, total,
    code1, land1, code2, land2, code3, land3, code4, land4, full, small_mine, small_land,
    local_sem, halo_send, halo_recv, pair_send, pair_recv, send1, recv1, send2, recv2,
    send3, recv3, send4, recv4, zsend, zrecv, qsend, qrecv, near_send, near_recv,
    far_send, far_recv, core_send, core_recv, small_send, small_recv, out_sem,
):
    dp, tm, rows = sizes
    frames, cols, chans = clips_ref.shape
    count = frames * cols
    me = {"dp": lax.axis_index("dp"), "tm": lax.axis_index("tm"), "rows": lax.axis_index("rows")}
    core = lax.rem(me["tm"], CORES)
    here = {
        "x": me["rows"],
        "y": 2 * me["dp"] + lax.rem(me["tm"] // 2, 2),
        "z": me["tm"] // 4,
        "c": core,
    }

    def device(**moved):
        place = dict(me, **moved)
        return (place["dp"], place["tm"], place["rows"])

    def chip(**moved):
        place = dict(here, **moved)
        return (
            place["y"] // 2,
            place["z"] * 4 + lax.rem(place["y"], 2) * 2 + place["c"],
            place["x"],
        )

    partner = chip(c=1 - core)

    def ring_peers(axis, size):
        return [lax.rem(here[axis] + step, size) for step in range(1, size)]

    weight_copy = pltpu.make_async_copy(weight_ref, w_ref, local_sem.at[0])
    weight_copy.start()
    shift = 2 * core
    clip_copy = pltpu.make_async_copy(
        clips_ref, clip_pad.at[pl.ds(shift + 1, frames), 1], local_sem.at[1]
    )
    clip_copy.start()
    for pad, base in ((clip_pad, shift), (score_pad, 0), (grad_pad, shift)):
        pad[pl.ds(base, frames + 2), 0] = jnp.zeros((frames + 2, cols, chans), pad.dtype)
        pad[pl.ds(base, frames + 2), 2] = jnp.zeros((frames + 2, cols, chans), pad.dtype)
        pad[base, 1] = jnp.zeros((cols, chans), pad.dtype)
        pad[base + frames + 1, 1] = jnp.zeros((cols, chans), pad.dtype)

    moves = [(t, r) for t in (-1, 0, 1) for r in (-1, 0, 1) if (t, r) != (0, 0)]

    def inside(t, r):
        ok = None
        for axis, step, size in (("tm", t, tm), ("rows", r, rows)):
            if step:
                cond = me[axis] > 0 if step < 0 else me[axis] < size - 1
                ok = cond if ok is None else jnp.logical_and(ok, cond)
        return ok

    barrier = pltpu.get_barrier_semaphore()
    friends = [partner]
    friends += [chip(x=other) for other in ring_peers("x", RING)]
    friends += [chip(y=other) for other in ring_peers("y", RING)]
    friends += [chip(z=other) for other in ring_peers("z", DEEP)]
    for friend in friends:
        pl.semaphore_signal(barrier, inc=1, device_id=friend, device_id_type=MESH)
    corners = [(t, r) for t, r in moves if t != 0]
    for t, r in corners:
        @pl.when(inside(t, r))
        def _():
            pl.semaphore_signal(
                barrier, inc=1, device_id=device(tm=me["tm"] + t, rows=me["rows"] + r),
                device_id_type=MESH,
            )
    expected = len(friends)
    for t, r in corners:
        expected = expected + inside(t, r).astype(jnp.int32)
    pl.semaphore_wait(barrier, expected)

    def halo_copy(which, pad, source, t, r):
        slot = which * len(moves) + moves.index((t, r))
        wide = pad.shape[0] > frames + 2
        base = 0
        if wide:
            base = shift if t == 0 else 2 - shift
        if t == 0:
            src, dst = pl.ds(0, frames), pl.ds(base + 1, frames)
        elif t > 0:
            src, dst = pl.ds(frames - 1, 1), pl.ds(base, 1)
        else:
            src, dst = pl.ds(0, 1), pl.ds(base + frames + 1, 1)
        return pltpu.make_async_remote_copy(
            src_ref=source.at[src], dst_ref=pad.at[dst, 1 - r],
            send_sem=halo_send.at[slot], recv_sem=halo_recv.at[slot],
            device_id=device(tm=me["tm"] + t, rows=me["rows"] + r), device_id_type=MESH,
        )

    def halo_start(which, pad, source):
        for t, r in sorted(moves, key=lambda move: move[0] != 0):
            @pl.when(inside(t, r))
            def _():
                halo_copy(which, pad, source, t, r).start()

    def halo_wait(which, pad, source, level):
        for t, r in moves:
            if (t == 0) != level:
                continue

            @pl.when(inside(t, r))
            def _():
                halo_copy(which, pad, source, t, r).wait_send()

            @pl.when(inside(-t, -r))
            def _():
                halo_copy(which, pad, source, t, r).wait_recv()

    column = lax.rem(lax.broadcasted_iota(jnp.int32, (count, chans), 0), cols)

    def earlier(value):
        return jnp.where(column == 0, 0.0, pltpu.roll(value, 1, 0))

    def later(value):
        return jnp.where(column == cols - 1, 0.0, pltpu.roll(value, count - 1, 0))

    def send(src, dst, send_sem, recv_sem, target):
        return pltpu.make_async_remote_copy(
            src_ref=src, dst_ref=dst, send_sem=send_sem, recv_sem=recv_sem,
            device_id=target, device_id_type=MESH,
        )

    def pair_frames(pad, slot):
        block = pad.at[pl.ds(4 * core, 2)]
        return send(block, block, pair_send.at[slot], pair_recv.at[slot], partner)

    def conv(which, pad, source, transpose, ready=None):
        base = shift if pad.shape[0] > frames + 2 else 0

        def step(a):
            at = base + ((TAPS - 1 - a) if transpose else a)
            pieces = [
                pad[pl.ds(at, frames), (TAPS - 1 - b) if transpose else b].reshape(count, chans)
                for b in range(TAPS)
            ]
            left = jnp.concatenate(pieces, axis=1)
            for d in range(TAPS):
                taps = [w_ref[(a * TAPS + b) * TAPS + d] for b in range(TAPS)]
                if transpose:
                    part = lax.dot_general(
                        left, jnp.concatenate(taps, axis=1), (((1,), (1,)), ((), ())),
                        preferred_element_type=jnp.float32,
                    )
                else:
                    part = jnp.dot(
                        left, jnp.concatenate(taps, axis=0), preferred_element_type=jnp.float32
                    )
                acc[d] = part if a == 1 else acc[d] + part

        halo_wait(which, pad, source, True)
        step(1)
        halo_wait(which, pad, source, False)
        if ready is not None:
            ready()
        step(0)
        step(2)
        if transpose:
            return later(acc[0]) + acc[1] + earlier(acc[2])
        return earlier(acc[0]) + acc[1] + later(acc[2])

    def split_pair(value, cat, stage, slot):
        value = value.astype(jnp.float32)
        three = [later(value), value, earlier(value)]
        low = jnp.concatenate([v[:, :LANES] for v in three], axis=1)
        high = jnp.concatenate([v[:, LANES:] for v in three], axis=1)
        first = core == 0
        cat[core] = jnp.where(first, low, high).astype(jnp.bfloat16)
        stage[...] = jnp.where(first, high, low).astype(jnp.bfloat16)
        copy = send(stage, cat.at[core], pair_send.at[slot], pair_recv.at[slot], partner)
        copy.start()
        return copy

    halo_start(0, clip_pad, clips_ref)
    clip_copy.wait()
    weight_copy.wait()
    pair_clips, pair_grads = pair_frames(clip_pad, 0), pair_frames(grad_pad, 1)
    pre = conv(0, clip_pad, clips_ref, False, pair_clips.start) + bias_ref[...]
    sig = jax.nn.sigmoid(pre)
    slope = sig * (1.0 + pre * (1.0 - sig))
    slope_ref[...] = slope
    curve_ref[...] = sig * (1.0 - sig) * (2.0 + pre * (1.0 - 2.0 * sig))
    score = (head_ref[...] * slope).astype(jnp.bfloat16)
    score_pad[pl.ds(1, frames), 1] = score.reshape(frames, cols, chans)
    score_own = score_pad.at[pl.ds(1, frames), 1]
    halo_start(1, score_pad, score_own)
    pair_s = split_pair(score, cat_s, stage_s, 2)

    input_grad = conv(1, score_pad, score_own, True).astype(jnp.bfloat16)
    grad_pad[pl.ds(shift + 1, frames), 1] = input_grad.reshape(frames, cols, chans)
    grad_own = grad_pad.at[pl.ds(shift + 1, frames), 1]
    halo_start(2, grad_pad, grad_own)

    back = penalty_weight * conv(2, grad_pad, grad_own, False, pair_grads.start)
    pre_grad = back * head_ref[...] * curve_ref[...]
    pair_p = split_pair(pre_grad.astype(jnp.bfloat16), cat_p, stage_p, 3)

    small_mine[...] = jnp.zeros_like(small_mine)
    for k, value in enumerate((pre_grad, back * slope_ref[...])):
        whole = jnp.sum(value, axis=0, keepdims=True)
        small_mine[pl.ds(2 * k, 1)] = whole[:, :LANES]
        small_mine[pl.ds(2 * k + 1, 1)] = whole[:, LANES:]
    small_targets = [
        [partner],
        [chip(x=other) for other in ring_peers("x", RING)],
        [chip(y=other) for other in ring_peers("y", RING)],
        [chip(z=other) for other in ring_peers("z", DEEP)],
    ]
    sent = []
    smalls = []

    def small_start(level):
        at = sum(len(group) for group in small_targets[:level])
        copies = []
        for k, target in enumerate(small_targets[level]):
            copy = send(
                small_mine.at[pl.ds(level * SUB, SUB)], small_land.at[pl.ds((at + k) * SUB, SUB)],
                small_send.at[at + k], small_recv.at[at + k], target,
            )
            copy.start()
            copies.append((copy, at + k))
        smalls.append(copies)

    def small_end(level):
        value = small_mine[pl.ds(level * SUB, SUB)]
        for copy, slot in smalls[level]:
            copy.wait_recv()
            sent.append(copy)
            value = value + small_land[pl.ds(slot * SUB, SUB)]
        small_mine[pl.ds((level + 1) * SUB, SUB)] = value

    small_start(0)

    routes = []
    for p in range(PARTS):
        first, second = ("x", "y") if p < GROUPS else ("y", "x")
        m, n = here[first], here[second]
        if p % 2 == 0:
            near, bit1, far, bit2 = flip(m), lax.rem((m + 1) // 2, 2), mirror(m), m // 2
        else:
            near, bit1, far, bit2 = mirror(m), m // 2, flip(m), lax.rem(m, 2)
        eight = 8 * bit1
        four = eight + 4 * bit2
        routes.append(dict(
            near=chip(**{first: near}), far=chip(**{first: far}),
            eight=eight, other8=8 - eight, four=four, other4=2 * eight + 4 - four,
            unit=four + n, second=second,
        ))

    def encode(p, base, units, code, at):
        def peak(k, top):
            for t in range(SHARE):
                top = jnp.maximum(top, jnp.abs(total[p, base + k, t]))
            return top

        zero = jnp.zeros((SUB, LANES), jnp.float32)
        top = peak(0, zero) if units == 1 else lax.fori_loop(0, units, peak, zero)
        top = (top * 1.01 + 1e-30).astype(jnp.bfloat16)
        rate = SPAN / top.astype(jnp.float32)
        code[(*at, units * SHARE)] = top

        def fill(k, carry):
            code[(*at, pl.ds(k * SHARE, SHARE))] = jnp.exp2(
                total[p, base + k] * rate[None]
            ).astype(jnp.bfloat16)
            return carry

        if units == 1:
            fill(0, 0)
        else:
            lax.fori_loop(0, units, fill, 0)

    def absorb(p, base, units, lands):
        scales = [
            land[(*at, units * SHARE)].astype(jnp.float32) * (1.0 / (SPAN * math.log(2.0)))
            for land, at in lands
        ]

        def add(k, carry):
            value = total[p, base + k]
            for (land, at), scale in zip(lands, scales):
                block = land[(*at, pl.ds(k * SHARE, SHARE))].astype(jnp.float32)
                value = value + jnp.log(block) * scale[None]
            total[p, base + k] = value
            return carry

        if units == 1:
            add(0, 0)
        else:
            lax.fori_loop(0, units, add, 0)

    def copy1(p):
        return send(code1.at[p], land1.at[p], send1.at[p], recv1.at[p], routes[p]["near"])

    def copy2(p):
        return send(code2.at[p], land2.at[p], send2.at[p], recv2.at[p], routes[p]["far"])

    def copy3(p):
        second = routes[p]["second"]
        return [
            send(
                code3.at[p, k], land3.at[p, k], send3.at[p * 3 + k], recv3.at[p * 3 + k],
                chip(**{second: other}),
            )
            for k, other in enumerate(ring_peers(second, RING))
        ]

    def start1(p):
        encode(p, routes[p]["other8"], 8, code1, (p,))
        copy1(p).start()
        sent.append(copy1(p))

    def start2(p):
        encode(p, routes[p]["other4"], 4, code2, (p,))
        copy2(p).start()
        sent.append(copy2(p))

    def start3(p):
        second = routes[p]["second"]
        for k, (copy, other) in enumerate(zip(copy3(p), ring_peers(second, RING))):
            encode(p, routes[p]["four"] + other, 1, code3, (p, k))
            copy.start()
            sent.append(copy)

    def correlate(pad, cat, a, b):
        left = pad[a : a + 2 * frames, b].reshape(2 * count, chans)
        right = cat[...].reshape(2 * count, TAPS * LANES)
        return lax.dot_general(
            left, right, (((0,), (0,)), ((), ())), preferred_element_type=jnp.float32
        )

    def tiles(value, h, d):
        block = value[h * UNITS * SUB : (h + 1) * UNITS * SUB, d * LANES : (d + 1) * LANES]
        return block.reshape(UNITS, SUB, LANES)

    def place(a, b, d):
        tap = (a * TAPS + b) * TAPS + d
        return tap // SHARE, tap % SHARE

    for h in range(2):
        total[h * GROUPS + GROUPS - 1, :, SHARE - 1] = jnp.zeros((UNITS, SUB, LANES), jnp.float32)
    pair_s.wait()
    pair_grads.wait()
    for b in range(TAPS):
        first = penalty_weight * correlate(grad_pad, cat_s, 0, b)
        for d in range(TAPS):
            g, t = place(0, b, d)
            for h in range(2):
                total[h * GROUPS + g, :, t] = tiles(first, h, d)
    pair_clips.wait()
    pair_p.wait()
    begun = 0
    for a in range(TAPS):
        for b in range(TAPS):
            value = correlate(clip_pad, cat_p, a, b)
            if a > 0:
                value = value + penalty_weight * correlate(grad_pad, cat_s, a, b)
            for d in range(TAPS):
                g, t = place(a, b, d)
                for h in range(2):
                    p = h * GROUPS + g
                    block = tiles(value, h, d)
                    total[p, :, t] = block + total[p, :, t] if a == 0 else block
            done = (a * TAPS + b + 1) * TAPS
            while begun < GROUPS and done >= min((begun + 1) * SHARE, TAPS**3):
                for h in range(2):
                    start1(h * GROUPS + begun)
                begun += 1

    small_end(0)
    small_start(1)
    order = [h * GROUPS + g for g in range(GROUPS) for h in range(2)]
    for p in order:
        copy1(p).wait_recv()
        absorb(p, routes[p]["eight"], 8, [(land1, (p,))])
        start2(p)
    small_end(1)
    small_start(2)
    for p in order:
        copy2(p).wait_recv()
        absorb(p, routes[p]["four"], 4, [(land2, (p,))])
        start3(p)
    small_end(2)
    small_start(3)

    z = here["z"]

    def copy4(p):
        return send(code4.at[p], land4.at[z], send4.at[p], recv4.at[z], chip(z=p))

    def got4(p):
        return send(code4.at[p], land4.at[p], send4.at[p], recv4.at[p], chip(z=p))

    for p in order:
        for copy in copy3(p):
            copy.wait_recv()
        absorb(p, routes[p]["unit"], 1, [(land3, (p, k)) for k in range(RING - 1)])

        @pl.when(z != p)
        def _():
            encode(p, routes[p]["unit"], 1, code4, (p,))
            copy4(p).start()

    unit = None
    for p in range(PARTS):
        term = jnp.where(z == p, routes[p]["unit"], 0)
        unit = term if unit is None else unit + term
    others = ring_peers("z", DEEP)
    for other in others:
        send(
            code4.at[other], land4.at[other], send4.at[other], recv4.at[other], chip(z=other)
        ).wait_recv()
    absorb(z, unit, 1, [(land4, (other,)) for other in others])
    encode(z, unit, 1, full, (z, core, unit))

    def zcopy(k, other):
        block = full.at[z, core, unit]
        return send(block, block, zsend.at[k], zrecv.at[z], chip(z=other))

    def zgot(p):
        block = full.at[p, core, routes[p]["unit"]]
        return send(block, block, zsend.at[0], zrecv.at[p], chip(z=p))

    for k, other in enumerate(others):
        zcopy(k, other).start()
        sent.append(zcopy(k, other))
    small_end(3)

    def qcopies(p):
        second = routes[p]["second"]
        block = full.at[p, core, routes[p]["unit"]]
        return [
            send(block, block, qsend.at[p * 3 + k], qrecv.at[p * 3 + k], chip(**{second: other}))
            for k, other in enumerate(ring_peers(second, RING))
        ]

    def far_copy(p):
        block = full.at[p, core, pl.ds(routes[p]["four"], 4)]
        return send(block, block, far_send.at[p], far_recv.at[p], routes[p]["far"])

    def near_copy(p):
        block = full.at[p, core, pl.ds(routes[p]["eight"], 8)]
        return send(block, block, near_send.at[p], near_recv.at[p], routes[p]["near"])

    def core_copy(p, second):
        base = routes[p]["other8"] if second else routes[p]["eight"]
        block = full.at[p, core, pl.ds(base, 8)]
        slot = 2 * p + second
        return send(block, block, core_send.at[slot], core_recv.at[slot], partner)

    for p in order:
        @pl.when(z != p)
        def _():
            zgot(p).wait_recv()

        for copy in qcopies(p):
            copy.start()
            sent.append(copy)
    for p in order:
        for copy in qcopies(p):
            copy.wait_recv()
        far_copy(p).start()
        sent.append(far_copy(p))
    for p in order:
        far_copy(p).wait_recv()
        near_copy(p).start()
        core_copy(p, 0).start()
        sent += [near_copy(p), core_copy(p, 0)]
    for p in order:
        near_copy(p).wait_recv()
        core_copy(p, 1).start()
        sent.append(core_copy(p, 1))
    for k, ref in enumerate((bias_out, head_out)):
        at = (len(small_targets)) * SUB + 2 * k
        ref[:, pl.ds(0, LANES)] = small_mine[pl.ds(at, 1)]
        ref[:, pl.ds(LANES, LANES)] = small_mine[pl.ds(at + 1, 1)]
    outs = []
    for p in order:
        core_copy(p, 0).wait_recv()
        core_copy(p, 1).wait_recv()
        copy = pltpu.make_async_copy(full.at[p], out_ref.at[p], out_sem.at[p])
        copy.start()
        outs.append(copy)
    for copy in sent:
        copy.wait_send()
    for p in range(PARTS):
        @pl.when(z != p)
        def _():
            copy4(p).wait_send()
    for copy in outs:
        copy.wait()


def decode_kernel(code_ref, bias_ref, head_ref, out_ref, bias_out, head_out):
    step = code_ref.shape[2]
    for g in range(GROUPS):
        taps = min(SHARE, TAPS**3 - g * SHARE)
        for c in range(CORES):
            for k in range(step):
                unit = code_ref[g, c, k, SHARE].astype(jnp.float32) * (1.0 / (SPAN * math.log(2.0)))
                block = code_ref[g, c, k, pl.ds(0, taps)].astype(jnp.float32)
                out_ref[pl.ds(g * SHARE, taps), k, :, pl.ds(c * LANES, LANES)] = (
                    jnp.log(block) * unit[None]
                )
    bias_out[...] = bias_ref[...]
    head_out[...] = head_ref[...]


def per_device(sizes, clips, weight, bias, head):
    _, frames, _, cols, chans = clips.shape
    count = frames * cols
    dp, tm, rows = sizes
    assert (rows, dp * 2, tm // 4, chans) == (RING, RING, DEEP, 2 * LANES)
    dma = pltpu.SemaphoreType.DMA
    vmem = pl.BlockSpec(memory_space=pltpu.VMEM)
    hbm = pl.BlockSpec(memory_space=pl.ANY)
    row = jax.ShapeDtypeStruct((1, chans), jnp.float32)
    field = pltpu.VMEM((count, chans), jnp.float32)

    def pad(n):
        return pltpu.VMEM((n, 3, cols, chans), jnp.bfloat16)

    def coded(*lead, units):
        return pltpu.VMEM((*lead, units * SHARE + 1, SUB, LANES), jnp.bfloat16)

    cat = pltpu.VMEM((CORES, count, TAPS * LANES), jnp.bfloat16)
    stage = pltpu.VMEM((count, TAPS * LANES), jnp.bfloat16)
    smalls = 1 + 2 * (RING - 1) + DEEP - 1
    both = lambda n: [dma((n,)), dma((n,))]
    code, *small = pl.pallas_call(
        functools.partial(kernel, sizes),
        out_shape=(
            jax.ShapeDtypeStruct((PARTS, CORES, UNITS, SHARE + 1, SUB, LANES), jnp.bfloat16),
            row, row,
        ),
        in_specs=[hbm, hbm, vmem, vmem],
        out_specs=(hbm, vmem, vmem),
        scratch_shapes=[
            pltpu.VMEM((TAPS**3, chans, chans), jnp.bfloat16),
            pad(2 * frames + 2), pad(frames + 2), pad(2 * frames + 2),
            pltpu.VMEM((TAPS, count, chans), jnp.float32),
            field, field,
            cat, cat, stage, stage,
            pltpu.VMEM((PARTS, UNITS, SHARE, SUB, LANES), jnp.float32),
            coded(PARTS, units=8), coded(PARTS, units=8),
            coded(PARTS, units=4), coded(PARTS, units=4),
            coded(PARTS, RING - 1, units=1), coded(PARTS, RING - 1, units=1),
            coded(DEEP, units=1), coded(DEEP, units=1),
            coded(PARTS, CORES, UNITS, units=1),
            pltpu.VMEM((5 * SUB, LANES), jnp.float32),
            pltpu.VMEM((smalls * SUB, LANES), jnp.float32),
            dma((2,)), *both(24), *both(4), *both(PARTS), *both(PARTS),
            *both(PARTS * 3), *both(DEEP), *both(DEEP), *both(PARTS * 3), *both(PARTS),
            *both(PARTS), *both(2 * PARTS), *both(smalls), dma((PARTS,)),
        ],
        compiler_params=pltpu.CompilerParams(
            collective_id=0, has_side_effects=True, vmem_limit_bytes=60 * 1024 * 1024
        ),
    )(
        clips.reshape(frames, cols, chans),
        weight.reshape(TAPS**3, chans, chans),
        bias.reshape(1, chans),
        head.reshape(1, chans),
    )
    step = 4
    turns = UNITS // step
    short = pl.BlockSpec((1, chans), lambda h, i: (0, 0))
    grad_weight, grad_bias, grad_head = pl.pallas_call(
        decode_kernel,
        out_shape=(jax.ShapeDtypeStruct((TAPS**3, 2 * UNITS, SUB, chans), jnp.float32), row, row),
        grid=(2, turns),
        in_specs=[
            pl.BlockSpec(
                (GROUPS, CORES, step, SHARE + 1, SUB, LANES), lambda h, i: (h, 0, i, 0, 0, 0)
            ),
            short, short,
        ],
        out_specs=(
            pl.BlockSpec((TAPS**3, step, SUB, chans), lambda h, i: (0, h * turns + i, 0, 0)),
            short, short,
        ),
    )(code, *small)
    grad_weight = grad_weight.reshape(TAPS, TAPS, TAPS, chans, chans)
    return grad_weight, grad_bias.reshape(chans), grad_head.reshape(chans)


def solution(mesh):
    sizes = tuple(mesh.shape[axis] for axis in ("dp", "tm", "rows"))
    return jax.shard_map(
        functools.partial(per_device, sizes),
        mesh=mesh,
        in_specs=(P("dp", "tm", "rows", None, None), P(), P(), P()),
        out_specs=(P(), P(), P()),
        check_vma=False,
    )
```

time: 124 us -> 93.9 us (0.76)
  Pallas kernels: 123 us -> 93 us
    pallas_call x1, Pallas kernels: 117 us -> 85.6 us  [per_device(): pl.pallas_call(functools.partial(kernel, sizes), out_shape=(jax.ShapeDtyp...]
    pallas_call x1, Pallas kernels: 5.79 us -> 7.39 us  [per_device(): pl.pallas_call(decode_kernel, out_shape=(jax.ShapeDtypeStruct((TAPS ** 3,...]
where the time goes in v2:
time: 93.9 us; the launch traced here: 93.6 us
  Pallas kernels  93 us (99%)
    pallas_call x1, Pallas kernels, per_device(): pl.pallas_call(functools.partial(kernel, sizes), out_shape=(jax.ShapeDtyp...  85.6 us
    pallas_call x1, Pallas kernels, per_device(): pl.pallas_call(decode_kernel, out_shape=(jax.ShapeDtypeStruct((TAPS ** 3,...  7.39 us

profile of v2, /device:TPU:1, one launch (start us, length us, event | category | flops | bytes accessed | tf_op | source)
XLA Modules:
  0.0 93.6 jit_solution(11614556409309907711)
XLA Ops:
  0.6 85.6 %shard_map.67 = (bf16[8,2,16,8,8,128]{5,4,3,2,1,0:T(8,128)(2,1)}, f32[1,256]{1,0:T(1,128)}, f32[1,256]{1,0:T(1,128)}) custom-call(bf16[2,128,256]{2,1,0:T(8,128)(2,1)} %bitcast.8, bf16[27,256,256]{2,1,0:T(8,128)(2,1)} %bitcast.7, f32[1,256]{1,0:T(1,128)} %bitcast.9, f32[1,256]{1,0:T(1,128)} %bitcast.10), custom_call_target="tpu_custom_call" | custom-call | tf_op jit(solution)/shard_map/pallas_call | solution.py:573
  86.2 7.4 %shard_map.68 = (f32[27,32,8,256]{3,2,1,0:T(8,128)}, f32[1,256]{1,0:T(1,128)}, f32[1,256]{1,0:T(1,128)}) custom-call(bf16[8,2,16,8,8,128]{5,4,3,2,1,0:T(8,128)(2,1)} %get-tuple-element.9.code_ref, f32[1,256]{1,0:T(1,128)} %get-tuple-element.10.bias_ref, f32[1,256]{1,0:T(1,128)} %get-tuple-element.11.head_ref), custom_call_target="tpu_custom_call" | custom-call | tf_op jit(solution)/shard_map/pallas_call | solution.py:611

commit v3 on v2

--- a/solution.py
+++ b/solution.py
@@ -32,14 +32,14 @@
 
 
 def kernel(
-    sizes, clips_ref, weight_ref, bias_ref, head_ref,
+    sizes, clips_ref, weight_ref, bias_hbm, head_hbm,
     out_ref, bias_out, head_out,
-    w_ref, clip_pad, score_pad, grad_pad, acc, slope_ref, curve_ref,
+    bias_ref, head_ref, w_ref, clip_pad, score_pad, grad_pad, acc, slope_ref, curve_ref,
     cat_s, cat_p, stage_s, stage_p, total,
     code1, land1, code2, land2, code3, land3, code4, land4, full, small_mine, small_land,
     local_sem, halo_send, halo_recv, pair_send, pair_recv, send1, recv1, send2, recv2,
     send3, recv3, send4, recv4, zsend, zrecv, qsend, qrecv, near_send, near_recv,
-    far_send, far_recv, core_send, core_recv, small_send, small_recv, out_sem,
+    far_send, far_recv, core_send, core_recv, small_send, small_recv,
 ):
     dp, tm, rows = sizes
     frames, cols, chans = clips_ref.shape
@@ -77,6 +77,10 @@
         clips_ref, clip_pad.at[pl.ds(shift + 1, frames), 1], local_sem.at[1]
     )
     clip_copy.start()
+    bias_copy = pltpu.make_async_copy(bias_hbm, bias_ref, local_sem.at[2])
+    head_copy = pltpu.make_async_copy(head_hbm, head_ref, local_sem.at[3])
+    bias_copy.start()
+    head_copy.start()
     for pad, base in ((clip_pad, shift), (score_pad, 0), (grad_pad, shift)):
         pad[pl.ds(base, frames + 2), 0] = jnp.zeros((frames + 2, cols, chans), pad.dtype)
         pad[pl.ds(base, frames + 2), 2] = jnp.zeros((frames + 2, cols, chans), pad.dtype)
@@ -217,6 +221,8 @@
     halo_start(0, clip_pad, clips_ref)
     clip_copy.wait()
     weight_copy.wait()
+    bias_copy.wait()
+    head_copy.wait()
     pair_clips, pair_grads = pair_frames(clip_pad, 0), pair_frames(grad_pad, 1)
     pre = conv(0, clip_pad, clips_ref, False, pair_clips.start) + bias_ref[...]
     sig = jax.nn.sigmoid(pre)
@@ -249,7 +255,6 @@
         [chip(y=other) for other in ring_peers("y", RING)],
         [chip(z=other) for other in ring_peers("z", DEEP)],
     ]
-    sent = []
     smalls = []
 
     def small_start(level):
@@ -258,17 +263,18 @@
         for k, target in enumerate(small_targets[level]):
             copy = send(
                 small_mine.at[pl.ds(level * SUB, SUB)], small_land.at[pl.ds((at + k) * SUB, SUB)],
-                small_send.at[at + k], small_recv.at[at + k], target,
+                small_send.at[0], small_recv.at[level], target,
             )
             copy.start()
-            copies.append((copy, at + k))
+            copies.append(at + k)
         smalls.append(copies)
 
     def small_end(level):
         value = small_mine[pl.ds(level * SUB, SUB)]
-        for copy, slot in smalls[level]:
-            copy.wait_recv()
-            sent.append(copy)
+        slots = smalls[level]
+        lands = small_land.at[pl.ds(slots[0] * SUB, len(slots) * SUB)]
+        send(lands, lands, small_send.at[0], small_recv.at[level], partner).wait_recv()
+        for slot in slots:
             value = value + small_land[pl.ds(slot * SUB, SUB)]
         small_mine[pl.ds((level + 1) * SUB, SUB)] = value
 
@@ -333,16 +339,16 @@
             lax.fori_loop(0, units, add, 0)
 
     def copy1(p):
-        return send(code1.at[p], land1.at[p], send1.at[p], recv1.at[p], routes[p]["near"])
+        return send(code1.at[p], land1.at[p], send1.at[0], recv1.at[p], routes[p]["near"])
 
     def copy2(p):
-        return send(code2.at[p], land2.at[p], send2.at[p], recv2.at[p], routes[p]["far"])
+        return send(code2.at[p], land2.at[p], send2.at[0], recv2.at[p], routes[p]["far"])
 
     def copy3(p):
         second = routes[p]["second"]
         return [
             send(
-                code3.at[p, k], land3.at[p, k], send3.at[p * 3 + k], recv3.at[p * 3 + k],
+                code3.at[p, k], land3.at[p, k], send3.at[0], recv3.at[p],
                 chip(**{second: other}),
             )
             for k, other in enumerate(ring_peers(second, RING))
@@ -351,19 +357,16 @@
     def start1(p):
         encode(p, routes[p]["other8"], 8, code1, (p,))
         copy1(p).start()
-        sent.append(copy1(p))
 
     def start2(p):
         encode(p, routes[p]["other4"], 4, code2, (p,))
         copy2(p).start()
-        sent.append(copy2(p))
 
     def start3(p):
         second = routes[p]["second"]
         for k, (copy, other) in enumerate(zip(copy3(p), ring_peers(second, RING))):
             encode(p, routes[p]["four"] + other, 1, code3, (p, k))
             copy.start()
-            sent.append(copy)
 
     def correlate(pad, cat, a, b):
         left = pad[a : a + 2 * frames, b].reshape(2 * count, chans)
@@ -429,14 +432,10 @@
     z = here["z"]
 
     def copy4(p):
-        return send(code4.at[p], land4.at[z], send4.at[p], recv4.at[z], chip(z=p))
-
-    def got4(p):
-        return send(code4.at[p], land4.at[p], send4.at[p], recv4.at[p], chip(z=p))
-
-    for p in order:
-        for copy in copy3(p):
-            copy.wait_recv()
+        return send(code4.at[p], land4.at[z], send4.at[0], recv4.at[0], chip(z=p))
+
+    for p in order:
+        send(land3.at[p], land3.at[p], send3.at[0], recv3.at[p], partner).wait_recv()
         absorb(p, routes[p]["unit"], 1, [(land3, (p, k)) for k in range(RING - 1)])
 
         @pl.when(z != p)
@@ -449,16 +448,14 @@
         term = jnp.where(z == p, routes[p]["unit"], 0)
         unit = term if unit is None else unit + term
     others = ring_peers("z", DEEP)
-    for other in others:
-        send(
-            code4.at[other], land4.at[other], send4.at[other], recv4.at[other], chip(z=other)
-        ).wait_recv()
+    seven = land4.at[pl.ds(0, DEEP - 1)]
+    send(seven, seven, send4.at[0], recv4.at[0], partner).wait_recv()
     absorb(z, unit, 1, [(land4, (other,)) for other in others])
     encode(z, unit, 1, full, (z, core, unit))
 
     def zcopy(k, other):
         block = full.at[z, core, unit]
-        return send(block, block, zsend.at[k], zrecv.at[z], chip(z=other))
+        return send(block, block, zsend.at[0], zrecv.at[z], chip(z=other))
 
     def zgot(p):
         block = full.at[p, core, routes[p]["unit"]]
@@ -466,30 +463,29 @@
 
     for k, other in enumerate(others):
         zcopy(k, other).start()
-        sent.append(zcopy(k, other))
     small_end(3)
 
     def qcopies(p):
         second = routes[p]["second"]
         block = full.at[p, core, routes[p]["unit"]]
         return [
-            send(block, block, qsend.at[p * 3 + k], qrecv.at[p * 3 + k], chip(**{second: other}))
+            send(block, block, qsend.at[0], qrecv.at[p], chip(**{second: other}))
             for k, other in enumerate(ring_peers(second, RING))
         ]
 
     def far_copy(p):
         block = full.at[p, core, pl.ds(routes[p]["four"], 4)]
-        return send(block, block, far_send.at[p], far_recv.at[p], routes[p]["far"])
+        return send(block, block, far_send.at[0], far_recv.at[p], routes[p]["far"])
 
     def near_copy(p):
         block = full.at[p, core, pl.ds(routes[p]["eight"], 8)]
-        return send(block, block, near_send.at[p], near_recv.at[p], routes[p]["near"])
+        return send(block, block, near_send.at[0], near_recv.at[p], routes[p]["near"])
 
     def core_copy(p, second):
         base = routes[p]["other8"] if second else routes[p]["eight"]
         block = full.at[p, core, pl.ds(base, 8)]
         slot = 2 * p + second
-        return send(block, block, core_send.at[slot], core_recv.at[slot], partner)
+        return send(block, block, core_send.at[0], core_recv.at[slot], partner)
 
     for p in order:
         @pl.when(z != p)
@@ -498,55 +494,67 @@
 
         for copy in qcopies(p):
             copy.start()
-            sent.append(copy)
-    for p in order:
-        for copy in qcopies(p):
-            copy.wait_recv()
+    for p in order:
+        three = full.at[p, core, pl.ds(0, RING - 1)]
+        send(three, three, qsend.at[0], qrecv.at[p], partner).wait_recv()
         far_copy(p).start()
-        sent.append(far_copy(p))
-    for p in order:
-        far_copy(p).wait_recv()
-        near_copy(p).start()
-        core_copy(p, 0).start()
-        sent += [near_copy(p), core_copy(p, 0)]
-    for p in order:
-        near_copy(p).wait_recv()
-        core_copy(p, 1).start()
-        sent.append(core_copy(p, 1))
+    def reveal(p, c, base):
+        h, g = p // GROUPS, p % GROUPS
+        taps = min(SHARE, TAPS**3 - g * SHARE)
+        lane = pl.ds(pl.multiple_of(c * LANES, LANES), LANES)
+
+        def one(k, carry):
+            scale = full[p, c, base + k, SHARE].astype(jnp.float32) * (1.0 / (SPAN * math.log(2.0)))
+            block = full[p, c, base + k, pl.ds(0, taps)].astype(jnp.float32)
+            out_ref[pl.ds(g * SHARE, taps), h * UNITS + base + k, :, lane] = (
+                jnp.log(block) * scale[None]
+            )
+            return carry
+
+        lax.fori_loop(0, 8, one, 0)
+
     for k, ref in enumerate((bias_out, head_out)):
         at = (len(small_targets)) * SUB + 2 * k
         ref[:, pl.ds(0, LANES)] = small_mine[pl.ds(at, 1)]
         ref[:, pl.ds(LANES, LANES)] = small_mine[pl.ds(at + 1, 1)]
-    outs = []
-    for p in order:
+    for p in order:
+        far_copy(p).wait_recv()
+        near_copy(p).start()
+        core_copy(p, 0).start()
+    for p in order:
+        reveal(p, core, routes[p]["eight"])
+        near_copy(p).wait_recv()
+        core_copy(p, 1).start()
+    for p in order:
+        reveal(p, core, routes[p]["other8"])
         core_copy(p, 0).wait_recv()
+        reveal(p, 1 - core, routes[p]["eight"])
+    for p in order:
         core_copy(p, 1).wait_recv()
-        copy = pltpu.make_async_copy(full.at[p], out_ref.at[p], out_sem.at[p])
+        reveal(p, 1 - core, routes[p]["other8"])
+    for block, sem in (
+        (small_land, small_send), (code1, send1), (code2, send2), (code3, send3),
+        (code4.at[pl.ds(0, DEEP - 1)], send4), (full.at[0, 0, pl.ds(0, DEEP - 1)], zsend),
+        (full.at[pl.ds(0, 3), 0, pl.ds(0, 8)], qsend), (full.at[0], far_send),
+        (full.at[pl.ds(0, 2)], near_send), (full.at[pl.ds(0, 4)], core_send),
+    ):
+        send(block, block, sem.at[0], sem.at[0], partner).wait_send()
+
+
+def store_kernel(grad_ref, bias_ref, head_ref, grad_out, bias_out, head_out, sem):
+    step = TAPS
+    copies = [
+        pltpu.make_async_copy(
+            grad_ref.at[pl.ds(k * step, step)], grad_out.at[pl.ds(k * step, step)], sem.at[k]
+        )
+        for k in range(TAPS**3 // step)
+    ]
+    copies.append(pltpu.make_async_copy(bias_ref, bias_out, sem.at[TAPS**2]))
+    copies.append(pltpu.make_async_copy(head_ref, head_out, sem.at[TAPS**2 + 1]))
+    for copy in copies:
         copy.start()
-        outs.append(copy)
-    for copy in sent:
-        copy.wait_send()
-    for p in range(PARTS):
-        @pl.when(z != p)
-        def _():
-            copy4(p).wait_send()
-    for copy in outs:
+    for copy in copies:
         copy.wait()
-
-
-def decode_kernel(code_ref, bias_ref, head_ref, out_ref, bias_out, head_out):
-    step = code_ref.shape[2]
-    for g in range(GROUPS):
-        taps = min(SHARE, TAPS**3 - g * SHARE)
-        for c in range(CORES):
-            for k in range(step):
-                unit = code_ref[g, c, k, SHARE].astype(jnp.float32) * (1.0 / (SPAN * math.log(2.0)))
-                block = code_ref[g, c, k, pl.ds(0, taps)].astype(jnp.float32)
-                out_ref[pl.ds(g * SHARE, taps), k, :, pl.ds(c * LANES, LANES)] = (
-                    jnp.log(block) * unit[None]
-                )
-    bias_out[...] = bias_ref[...]
-    head_out[...] = head_ref[...]
 
 
 def per_device(sizes, clips, weight, bias, head):
@@ -556,7 +564,7 @@
     assert (rows, dp * 2, tm // 4, chans) == (RING, RING, DEEP, 2 * LANES)
     dma = pltpu.SemaphoreType.DMA
     vmem = pl.BlockSpec(memory_space=pltpu.VMEM)
-    hbm = pl.BlockSpec(memory_space=pl.ANY)
+    hbm = pl.BlockSpec(memory_space=pltpu.HBM)
     row = jax.ShapeDtypeStruct((1, chans), jnp.float32)
     field = pltpu.VMEM((count, chans), jnp.float32)
 
@@ -570,15 +578,17 @@
     stage = pltpu.VMEM((count, TAPS * LANES), jnp.bfloat16)
     smalls = 1 + 2 * (RING - 1) + DEEP - 1
     both = lambda n: [dma((n,)), dma((n,))]
-    code, *small = pl.pallas_call(
+    one = lambda n: [dma((1,)), dma((n,))]
+    grad_weight, grad_bias, grad_head = pl.pallas_call(
         functools.partial(kernel, sizes),
         out_shape=(
-            jax.ShapeDtypeStruct((PARTS, CORES, UNITS, SHARE + 1, SUB, LANES), jnp.bfloat16),
+            jax.ShapeDtypeStruct((TAPS**3, 2 * UNITS, SUB, chans), jnp.float32),
             row, row,
         ),
-        in_specs=[hbm, hbm, vmem, vmem],
-        out_specs=(hbm, vmem, vmem),
+        in_specs=[hbm, hbm, hbm, hbm],
+        out_specs=(vmem, vmem, vmem),
         scratch_shapes=[
+            pltpu.VMEM((1, chans), jnp.float32), pltpu.VMEM((1, chans), jnp.float32),
             pltpu.VMEM((TAPS**3, chans, chans), jnp.bfloat16),
             pad(2 * frames + 2), pad(frames + 2), pad(2 * frames + 2),
             pltpu.VMEM((TAPS, count, chans), jnp.float32),
@@ -592,37 +602,31 @@
             coded(PARTS, CORES, UNITS, units=1),
             pltpu.VMEM((5 * SUB, LANES), jnp.float32),
             pltpu.VMEM((smalls * SUB, LANES), jnp.float32),
-            dma((2,)), *both(24), *both(4), *both(PARTS), *both(PARTS),
-            *both(PARTS * 3), *both(DEEP), *both(DEEP), *both(PARTS * 3), *both(PARTS),
-            *both(PARTS), *both(2 * PARTS), *both(smalls), dma((PARTS,)),
+            dma((4,)), *both(24), *both(4), *one(PARTS), *one(PARTS), *one(PARTS), *one(1),
+            *one(DEEP), *one(PARTS), *one(PARTS), *one(PARTS), *one(2 * PARTS), *one(4),
         ],
         compiler_params=pltpu.CompilerParams(
-            collective_id=0, has_side_effects=True, vmem_limit_bytes=60 * 1024 * 1024
+            collective_id=0, has_side_effects=True, vmem_limit_bytes=40 * 1024 * 1024
         ),
     )(
-        clips.reshape(frames, cols, chans),
-        weight.reshape(TAPS**3, chans, chans),
-        bias.reshape(1, chans),
-        head.reshape(1, chans),
+        *[
+            pltpu.with_memory_space_constraint(value, pltpu.HBM)
+            for value in (
+                clips.reshape(frames, cols, chans), weight.reshape(TAPS**3, chans, chans),
+                bias.reshape(1, chans), head.reshape(1, chans),
+            )
+        ]
     )
-    step = 4
-    turns = UNITS // step
-    short = pl.BlockSpec((1, chans), lambda h, i: (0, 0))
     grad_weight, grad_bias, grad_head = pl.pallas_call(
-        decode_kernel,
-        out_shape=(jax.ShapeDtypeStruct((TAPS**3, 2 * UNITS, SUB, chans), jnp.float32), row, row),
-        grid=(2, turns),
-        in_specs=[
-            pl.BlockSpec(
-                (GROUPS, CORES, step, SHARE + 1, SUB, LANES), lambda h, i: (h, 0, i, 0, 0, 0)
-            ),
-            short, short,
-        ],
-        out_specs=(
-            pl.BlockSpec((TAPS**3, step, SUB, chans), lambda h, i: (0, h * turns + i, 0, 0)),
-            short, short,
+        store_kernel,
+        out_shape=(
+            jax.ShapeDtypeStruct((TAPS**3, 2 * UNITS, SUB, chans), jnp.float32), row, row,
         ),
-    )(code, *small)
+        in_specs=[vmem, vmem, vmem],
+        out_specs=(hbm, hbm, hbm),
+        scratch_shapes=[dma((TAPS**2 + 2,))],
+        compiler_params=pltpu.CompilerParams(vmem_limit_bytes=8 * 1024 * 1024),
+    )(grad_weight, grad_bias, grad_head)
     grad_weight = grad_weight.reshape(TAPS, TAPS, TAPS, chans, chans)
     return grad_weight, grad_bias.reshape(chans), grad_head.reshape(chans)
 

time: 93.9 us -> 85.9 us (0.915)
  Pallas kernels: 93 us -> 85.1 us
    pallas_call x1, Pallas kernels: 7.39 us -> 3.01 us  [per_device(): pl.pallas_call(store_kernel, out_shape=(jax.ShapeDtypeStruct((TAPS ** 3,...]
    pallas_call x1, Pallas kernels: 85.6 us -> 82 us  [per_device(): pl.pallas_call(functools.partial(kernel, sizes), out_shape=(jax.ShapeDtyp...]
where the time goes in v3:
time: 85.9 us; the launch traced here: 85.7 us
  Pallas kernels  85.1 us (99%)
    pallas_call x1, Pallas kernels, per_device(): pl.pallas_call(functools.partial(kernel, sizes), out_shape=(jax.ShapeDtyp...  82 us
    pallas_call x1, Pallas kernels, per_device(): pl.pallas_call(store_kernel, out_shape=(jax.ShapeDtypeStruct((TAPS ** 3,...  3.01 us

profile of v3, /device:TPU:1, one launch (start us, length us, event | category | flops | bytes accessed | tf_op | source)
XLA Modules:
  0.0 85.7 jit_solution(3165399561608538213)
XLA Ops:
  0.6 82.0 %shard_map.67 = (f32[27,32,8,256]{3,2,1,0:T(8,128)S(1)}, f32[1,256]{1,0:T(1,128)S(1)}, f32[1,256]{1,0:T(1,128)S(1)}) custom-call(bf16[2,128,256]{2,1,0:T(8,128)(2,1)} %bitcast.8, bf16[27,256,256]{2,1,0:T(8,128)(2,1)} %bitcast.7, f32[1,256]{1,0:T(1,128)} %bitcast.9, f32[1,256]{1,0:T(1,128)} %bitcast.10), custom_call_target="tpu_custom_call" | custom-call | tf_op jit(solution)/shard_map/pallas_call | solution.py:582
  82.7 3.0 %shard_map.68 = (f32[27,32,8,256]{3,2,1,0:T(8,128)}, f32[1,256]{1,0:T(1,128)}, f32[1,256]{1,0:T(1,128)}) custom-call(f32[27,32,8,256]{3,2,1,0:T(8,128)S(1)} %get-tuple-element.9.grad_ref, f32[1,256]{1,0:T(1,128)S(1)} %get-tuple-element.10.bias_ref, f32[1,256]{1,0:T(1,128)S(1)} %get-tuple-element.11.head_ref), custom_call_target="tpu_custom_call" | custom-call | tf_op jit(solution)/shard_map/pallas_call | solution.py:620

commit v4 on v3

--- a/solution.py
+++ b/solution.py
@@ -34,16 +34,20 @@
 def kernel(
     sizes, clips_ref, weight_ref, bias_hbm, head_hbm,
     out_ref, bias_out, head_out,
-    bias_ref, head_ref, w_ref, clip_pad, score_pad, grad_pad, acc, slope_ref, curve_ref,
-    cat_s, cat_p, stage_s, stage_p, total,
+    bias_ref, head_ref, w_ref, clips_vm, clip_pad, score_pad, grad_pad, acc, slope_ref, curve_ref,
+    cat_s, cat_p, stage_s, stage_p, raw_p, edge_out, edge_in, last_out, last_in, total,
     code1, land1, code2, land2, code3, land3, code4, land4, full, small_mine, small_land,
-    local_sem, halo_send, halo_recv, pair_send, pair_recv, send1, recv1, send2, recv2,
+    local_sem, turn_send, turn_recv, halo_send, halo_recv, last_send, last_recv,
+    pair_send, pair_recv, send1, recv1, send2, recv2,
     send3, recv3, send4, recv4, zsend, zrecv, qsend, qrecv, near_send, near_recv,
     far_send, far_recv, core_send, core_recv, small_send, small_recv,
 ):
     dp, tm, rows = sizes
-    frames, cols, chans = clips_ref.shape
-    count = frames * cols
+    frames, wide, chans = clips_ref.shape
+    cols = wide // RING
+    lines = frames * RING
+    count = lines * cols
+    half = count // 2
     me = {"dp": lax.axis_index("dp"), "tm": lax.axis_index("tm"), "rows": lax.axis_index("rows")}
     core = lax.rem(me["tm"], CORES)
     here = {
@@ -73,19 +77,19 @@
     weight_copy = pltpu.make_async_copy(weight_ref, w_ref, local_sem.at[0])
     weight_copy.start()
     shift = 2 * core
-    clip_copy = pltpu.make_async_copy(
-        clips_ref, clip_pad.at[pl.ds(shift + 1, frames), 1], local_sem.at[1]
-    )
+    clip_copy = pltpu.make_async_copy(clips_ref, clips_vm, local_sem.at[1])
     clip_copy.start()
     bias_copy = pltpu.make_async_copy(bias_hbm, bias_ref, local_sem.at[2])
     head_copy = pltpu.make_async_copy(head_hbm, head_ref, local_sem.at[3])
     bias_copy.start()
     head_copy.start()
     for pad, base in ((clip_pad, shift), (score_pad, 0), (grad_pad, shift)):
-        pad[pl.ds(base, frames + 2), 0] = jnp.zeros((frames + 2, cols, chans), pad.dtype)
-        pad[pl.ds(base, frames + 2), 2] = jnp.zeros((frames + 2, cols, chans), pad.dtype)
-        pad[base, 1] = jnp.zeros((cols, chans), pad.dtype)
-        pad[base + frames + 1, 1] = jnp.zeros((cols, chans), pad.dtype)
+        pad[:, 0] = jnp.zeros((pad.shape[0], cols, chans), pad.dtype)
+        pad[:, RING + 1] = jnp.zeros((pad.shape[0], cols, chans), pad.dtype)
+        for at in (base, base + frames + 1):
+            pad[at, pl.ds(1, RING)] = jnp.zeros((RING, cols, chans), pad.dtype)
+    edge_in[...] = jnp.zeros_like(edge_in)
+    last_in[...] = jnp.zeros_like(last_in)
 
     moves = [(t, r) for t in (-1, 0, 1) for r in (-1, 0, 1) if (t, r) != (0, 0)]
 
@@ -104,63 +108,18 @@
     friends += [chip(z=other) for other in ring_peers("z", DEEP)]
     for friend in friends:
         pl.semaphore_signal(barrier, inc=1, device_id=friend, device_id_type=MESH)
-    corners = [(t, r) for t, r in moves if t != 0]
-    for t, r in corners:
-        @pl.when(inside(t, r))
+    expected = len(friends)
+    for t in (-1, 1):
+        expected = expected + RING * inside(t, 0).astype(jnp.int32)
+
+        @pl.when(inside(t, 0))
         def _():
-            pl.semaphore_signal(
-                barrier, inc=1, device_id=device(tm=me["tm"] + t, rows=me["rows"] + r),
-                device_id_type=MESH,
-            )
-    expected = len(friends)
-    for t, r in corners:
-        expected = expected + inside(t, r).astype(jnp.int32)
+            for row in range(RING):
+                pl.semaphore_signal(
+                    barrier, inc=1, device_id=device(tm=me["tm"] + t, rows=row),
+                    device_id_type=MESH,
+                )
     pl.semaphore_wait(barrier, expected)
-
-    def halo_copy(which, pad, source, t, r):
-        slot = which * len(moves) + moves.index((t, r))
-        wide = pad.shape[0] > frames + 2
-        base = 0
-        if wide:
-            base = shift if t == 0 else 2 - shift
-        if t == 0:
-            src, dst = pl.ds(0, frames), pl.ds(base + 1, frames)
-        elif t > 0:
-            src, dst = pl.ds(frames - 1, 1), pl.ds(base, 1)
-        else:
-            src, dst = pl.ds(0, 1), pl.ds(base + frames + 1, 1)
-        return pltpu.make_async_remote_copy(
-            src_ref=source.at[src], dst_ref=pad.at[dst, 1 - r],
-            send_sem=halo_send.at[slot], recv_sem=halo_recv.at[slot],
-            device_id=device(tm=me["tm"] + t, rows=me["rows"] + r), device_id_type=MESH,
-        )
-
-    def halo_start(which, pad, source):
-        for t, r in sorted(moves, key=lambda move: move[0] != 0):
-            @pl.when(inside(t, r))
-            def _():
-                halo_copy(which, pad, source, t, r).start()
-
-    def halo_wait(which, pad, source, level):
-        for t, r in moves:
-            if (t == 0) != level:
-                continue
-
-            @pl.when(inside(t, r))
-            def _():
-                halo_copy(which, pad, source, t, r).wait_send()
-
-            @pl.when(inside(-t, -r))
-            def _():
-                halo_copy(which, pad, source, t, r).wait_recv()
-
-    column = lax.rem(lax.broadcasted_iota(jnp.int32, (count, chans), 0), cols)
-
-    def earlier(value):
-        return jnp.where(column == 0, 0.0, pltpu.roll(value, 1, 0))
-
-    def later(value):
-        return jnp.where(column == cols - 1, 0.0, pltpu.roll(value, count - 1, 0))
 
     def send(src, dst, send_sem, recv_sem, target):
         return pltpu.make_async_remote_copy(
@@ -168,81 +127,259 @@
             device_id=target, device_id_type=MESH,
         )
 
+    def turn_copy(t, step):
+        other = lax.rem(me["rows"] + step, RING)
+        part = pl.ds(pl.multiple_of(other * cols, cols), cols)
+        base = shift if t == 0 else 2 - shift
+        src = {0: pl.ds(0, frames), 1: pl.ds(frames - 1, 1), -1: pl.ds(0, 1)}[t]
+        dst = {0: pl.ds(base + 1, frames), 1: pl.ds(base, 1), -1: pl.ds(base + frames + 1, 1)}[t]
+        return send(
+            clips_vm.at[src, part], clip_pad.at[dst, 1 + me["rows"]],
+            turn_send.at[1 + t], turn_recv.at[1 + t],
+            device(tm=me["tm"] + t, rows=other),
+        )
+
+    def turn_start():
+        for step in range(1, RING):
+            turn_copy(0, step).start()
+        for t in (-1, 1):
+            @pl.when(inside(t, 0))
+            def _():
+                for step in range(RING):
+                    turn_copy(t, step).start()
+
+    def turn_wait(level):
+        if level:
+            block = clip_pad.at[pl.ds(shift + 1, frames), pl.ds(1, RING - 1)]
+            copy = send(block, block, turn_send.at[1], turn_recv.at[1], partner)
+            copy.wait_recv()
+            copy.wait_send()
+            return
+        for t in (-1, 1):
+            block = clip_pad.at[shift, pl.ds(1, RING)]
+            copy = send(block, block, turn_send.at[1 + t], turn_recv.at[1 + t], partner)
+
+            @pl.when(inside(t, 0))
+            def _():
+                copy.wait_send()
+
+            @pl.when(inside(-t, 0))
+            def _():
+                copy.wait_recv()
+
+    def halo_copy(which, pad, t, r):
+        slot = which * len(moves) + moves.index((t, r))
+        target = device(tm=me["tm"] + t, rows=me["rows"] + r)
+        sems = halo_send.at[slot], halo_recv.at[slot]
+        if r != 0:
+            side = 0 if r > 0 else 1
+            return send(edge_out.at[which, side], edge_in.at[which, side, 1 - t], *sems, target)
+        pair = pad.shape[0] > frames + 2
+        mine, base = (shift, 2 - shift) if pair else (0, 0)
+        src = mine + frames if t > 0 else mine + 1
+        dst = base if t > 0 else base + frames + 1
+        return send(
+            pad.at[src, pl.ds(1, RING)], pad.at[dst, pl.ds(1, RING)], *sems, target
+        )
+
+    def edge_rows(value):
+        block = value.reshape(lines, cols, value.shape[-1])
+        return block[:, cols - 1], block[:, 0]
+
+    def halo_start(which, pad, value, skip=False):
+        for side, rows_out in enumerate(edge_rows(value)):
+            edge_out[which, side] = rows_out
+        for t, r in sorted(moves, key=lambda move: move[1] != 0):
+            if skip and r == 0:
+                continue
+
+            @pl.when(inside(t, r))
+            def _():
+                halo_copy(which, pad, t, r).start()
+
+    def halo_wait(which, pad, skip=False):
+        for t, r in moves:
+            if skip and r == 0:
+                continue
+
+            @pl.when(inside(t, r))
+            def _():
+                halo_copy(which, pad, t, r).wait_send()
+
+            @pl.when(inside(-t, -r))
+            def _():
+                halo_copy(which, pad, t, r).wait_recv()
+
+    def columns(value):
+        return lax.rem(lax.broadcasted_iota(jnp.int32, value.shape, 0), cols)
+
+    def spread(edge):
+        return jnp.broadcast_to(edge[:, None, :], (lines, cols, edge.shape[-1])).reshape(count, -1)
+
+    def earlier(value, edge):
+        return jnp.where(columns(value) == 0, spread(edge), pltpu.roll(value, 1, 0))
+
+    def later(value, edge):
+        return jnp.where(columns(value) == cols - 1, spread(edge), pltpu.roll(value, count - 1, 0))
+
     def pair_frames(pad, slot):
-        block = pad.at[pl.ds(4 * core, 2)]
+        block = pad.at[pl.ds(4 * core, 2), pl.ds(1, RING)]
         return send(block, block, pair_send.at[slot], pair_recv.at[slot], partner)
 
-    def conv(which, pad, source, transpose, ready=None):
+    def edge_left(which):
+        line = lax.broadcasted_iota(jnp.int32, (lines, chans), 0)
+        row = lax.rem(line, RING)
+
+        def piece(side, s, q):
+            below, level, above = (edge_in[which, side, k] for k in range(3))
+            if s == 1:
+                value = level
+            else:
+                value = pltpu.roll(level, RING, 0)
+                if s == 0:
+                    value = jnp.where(line < RING, pltpu.roll(below, RING, 0), value)
+                else:
+                    value = jnp.where(line < RING, value, pltpu.roll(above, RING, 0))
+            if q == 0:
+                value = jnp.where(row == 0, 0.0, pltpu.roll(value, 1, 0))
+            elif q == 2:
+                value = jnp.where(row == RING - 1, 0.0, pltpu.roll(value, lines - 1, 0))
+            return value
+
+        return [
+            jnp.concatenate([
+                jnp.concatenate([piece(side, s, q) for q in range(TAPS)], axis=1)
+                for side in range(2)
+            ], axis=0).astype(jnp.bfloat16)
+            for s in range(TAPS)
+        ]
+
+    def conv(which, pad, transpose, wait, ready):
         base = shift if pad.shape[0] > frames + 2 else 0
 
-        def step(a):
-            at = base + ((TAPS - 1 - a) if transpose else a)
-            pieces = [
-                pad[pl.ds(at, frames), (TAPS - 1 - b) if transpose else b].reshape(count, chans)
-                for b in range(TAPS)
+        def left(at, size):
+            return jnp.concatenate([
+                pad[pl.ds(base + at, size), pl.ds(q, RING)].reshape(size * half, chans)
+                for q in range(TAPS)
+            ], axis=1)
+
+        def product(value, s, d):
+            a = TAPS - 1 - s if transpose else s
+            taps = [
+                w_ref[(a * TAPS + (TAPS - 1 - q if transpose else q)) * TAPS + d]
+                for q in range(TAPS)
             ]
-            left = jnp.concatenate(pieces, axis=1)
-            for d in range(TAPS):
-                taps = [w_ref[(a * TAPS + b) * TAPS + d] for b in range(TAPS)]
-                if transpose:
-                    part = lax.dot_general(
-                        left, jnp.concatenate(taps, axis=1), (((1,), (1,)), ((), ())),
-                        preferred_element_type=jnp.float32,
-                    )
-                else:
-                    part = jnp.dot(
-                        left, jnp.concatenate(taps, axis=0), preferred_element_type=jnp.float32
-                    )
-                acc[d] = part if a == 1 else acc[d] + part
-
-        halo_wait(which, pad, source, True)
-        step(1)
-        halo_wait(which, pad, source, False)
-        if ready is not None:
-            ready()
-        step(0)
-        step(2)
-        if transpose:
-            return later(acc[0]) + acc[1] + earlier(acc[2])
-        return earlier(acc[0]) + acc[1] + later(acc[2])
-
-    def split_pair(value, cat, stage, slot):
-        value = value.astype(jnp.float32)
-        three = [later(value), value, earlier(value)]
-        low = jnp.concatenate([v[:, :LANES] for v in three], axis=1)
-        high = jnp.concatenate([v[:, LANES:] for v in three], axis=1)
-        first = core == 0
-        cat[core] = jnp.where(first, low, high).astype(jnp.bfloat16)
-        stage[...] = jnp.where(first, high, low).astype(jnp.bfloat16)
-        copy = send(stage, cat.at[core], pair_send.at[slot], pair_recv.at[slot], partner)
-        copy.start()
-        return copy
-
-    halo_start(0, clip_pad, clips_ref)
+            if transpose:
+                return lax.dot_general(
+                    value, jnp.concatenate(taps, axis=1), (((1,), (1,)), ((), ())),
+                    preferred_element_type=jnp.float32,
+                )
+            return jnp.dot(
+                value, jnp.concatenate(taps, axis=0), preferred_element_type=jnp.float32
+            )
+
+        own = left(1, frames)
+        for d in range(TAPS):
+            level = product(own, 1, d)
+            acc[d, pl.ds(0, half)] = level[:half] + product(own[half:], 2, d)
+            acc[d, pl.ds(half, half)] = level[half:] + product(own[:half], 0, d)
+        wait()
+        ready()
+        edges = edge_left(which)
+        below = jnp.concatenate([left(0, 1), edges[0]], axis=0)
+        above = jnp.concatenate([left(frames + 1, 1), edges[2]], axis=0)
+        sums, sides = [], []
+        for d in range(TAPS):
+            low, high = product(below, 0, d), product(above, 2, d)
+            sums.append(jnp.concatenate([
+                acc[d, pl.ds(0, half)] + low[:half], acc[d, pl.ds(half, half)] + high[:half]
+            ], axis=0))
+            sides.append(
+                None if d == 1 else low[half:] + high[half:] + product(edges[1], 1, d)
+            )
+        d0, d2 = (2, 0) if transpose else (0, 2)
+        return (
+            earlier(sums[d0], sides[d0][:lines]) + sums[1] + later(sums[d2], sides[d2][lines:])
+        )
+
+
+    def lane_half(value, mine=True):
+        low, high = value[:, :LANES], value[:, LANES:]
+        return jnp.where(core == 0, low, high) if mine else jnp.where(core == 0, high, low)
+
+    def three(value, before, after):
+        return jnp.concatenate(
+            [later(value, after), value, earlier(value, before)], axis=1
+        ).astype(jnp.bfloat16)
+
     clip_copy.wait()
+    turn_start()
+    mine = pl.ds(pl.multiple_of(me["rows"] * cols, cols), cols)
+    clip_pad[pl.ds(shift + 1, frames), 1 + me["rows"]] = clips_vm[:, mine]
     weight_copy.wait()
     bias_copy.wait()
     head_copy.wait()
     pair_clips, pair_grads = pair_frames(clip_pad, 0), pair_frames(grad_pad, 1)
-    pre = conv(0, clip_pad, clips_ref, False, pair_clips.start) + bias_ref[...]
+    turn_wait(True)
+    clips = clip_pad[pl.ds(shift + 1, frames), pl.ds(1, RING)].reshape(count, chans)
+    halo_start(0, clip_pad, clips.astype(jnp.float32), True)
+
+    def wait_clips():
+        turn_wait(False)
+        halo_wait(0, clip_pad, True)
+
+    pre = conv(0, clip_pad, False, wait_clips, pair_clips.start) + bias_ref[...]
     sig = jax.nn.sigmoid(pre)
     slope = sig * (1.0 + pre * (1.0 - sig))
     slope_ref[...] = slope
     curve_ref[...] = sig * (1.0 - sig) * (2.0 + pre * (1.0 - 2.0 * sig))
     score = (head_ref[...] * slope).astype(jnp.bfloat16)
-    score_pad[pl.ds(1, frames), 1] = score.reshape(frames, cols, chans)
-    score_own = score_pad.at[pl.ds(1, frames), 1]
-    halo_start(1, score_pad, score_own)
-    pair_s = split_pair(score, cat_s, stage_s, 2)
-
-    input_grad = conv(1, score_pad, score_own, True).astype(jnp.bfloat16)
-    grad_pad[pl.ds(shift + 1, frames), 1] = input_grad.reshape(frames, cols, chans)
-    grad_own = grad_pad.at[pl.ds(shift + 1, frames), 1]
-    halo_start(2, grad_pad, grad_own)
-
-    back = penalty_weight * conv(2, grad_pad, grad_own, False, pair_grads.start)
+    score_pad[pl.ds(1, frames), pl.ds(1, RING)] = score.reshape(frames, RING, cols, chans)
+    halo_start(1, score_pad, score.astype(jnp.float32))
+
+    input_grad = conv(
+        1, score_pad, True, lambda: halo_wait(1, score_pad), lambda: None
+    ).astype(jnp.bfloat16)
+    grad_pad[pl.ds(shift + 1, frames), pl.ds(1, RING)] = input_grad.reshape(
+        frames, RING, cols, chans
+    )
+    halo_start(2, grad_pad, input_grad.astype(jnp.float32))
+
+    value = score_pad[pl.ds(1, frames), pl.ds(1, RING)].reshape(count, chans).astype(jnp.float32)
+    for mine, ref in ((True, cat_s.at[core]), (False, stage_s)):
+        ref[...] = three(
+            lane_half(value, mine),
+            lane_half(edge_in[1, 0, 1], mine), lane_half(edge_in[1, 1, 1], mine),
+        )
+    pair_s = send(stage_s, cat_s.at[core], pair_send.at[2], pair_recv.at[2], partner)
+    pair_s.start()
+
+    back = penalty_weight * conv(
+        2, grad_pad, False, lambda: halo_wait(2, grad_pad), pair_grads.start
+    )
     pre_grad = back * head_ref[...] * curve_ref[...]
-    pair_p = split_pair(pre_grad.astype(jnp.bfloat16), cat_p, stage_p, 3)
+    value = pre_grad.astype(jnp.bfloat16).astype(jnp.float32)
+    for side, rows_out in enumerate(edge_rows(value)):
+        last_out[side] = rows_out
+    stage_p[...] = lane_half(value, False).astype(jnp.bfloat16)
+    pair_p = send(stage_p, raw_p.at[1], pair_send.at[3], pair_recv.at[3], partner)
+    pair_p.start()
+    raw_p[0] = lane_half(value).astype(jnp.bfloat16)
+
+    def last_copy(r, c):
+        side = 0 if r > 0 else 1
+        slot = 2 * side + c
+        other = core if c == 0 else 1 - core
+        return send(
+            last_out.at[side], last_in.at[side, c], last_send.at[slot], last_recv.at[slot],
+            device(tm=me["tm"] - core + other, rows=me["rows"] + r),
+        )
+
+    for r in (-1, 1):
+        @pl.when(inside(0, r))
+        def _():
+            for c in range(CORES):
+                last_copy(r, c).start()
 
     small_mine[...] = jnp.zeros_like(small_mine)
     for k, value in enumerate((pre_grad, back * slope_ref[...])):
@@ -369,7 +506,7 @@
             copy.start()
 
     def correlate(pad, cat, a, b):
-        left = pad[a : a + 2 * frames, b].reshape(2 * count, chans)
+        left = pad[a : a + 2 * frames, b : b + RING].reshape(2 * count, chans)
         right = cat[...].reshape(2 * count, TAPS * LANES)
         return lax.dot_general(
             left, right, (((0,), (0,)), ((), ())), preferred_element_type=jnp.float32
@@ -387,26 +524,40 @@
         total[h * GROUPS + GROUPS - 1, :, SHARE - 1] = jnp.zeros((UNITS, SUB, LANES), jnp.float32)
     pair_s.wait()
     pair_grads.wait()
-    for b in range(TAPS):
-        first = penalty_weight * correlate(grad_pad, cat_s, 0, b)
-        for d in range(TAPS):
-            g, t = place(0, b, d)
-            for h in range(2):
-                total[h * GROUPS + g, :, t] = tiles(first, h, d)
+    for a in range(TAPS):
+        for b in range(TAPS):
+            value = penalty_weight * correlate(grad_pad, cat_s, a, b)
+            for d in range(TAPS):
+                g, t = place(a, b, d)
+                for h in range(2):
+                    total[h * GROUPS + g, :, t] = tiles(value, h, d)
     pair_clips.wait()
     pair_p.wait()
+    for r in (-1, 1):
+        for c in range(CORES):
+            @pl.when(inside(0, r))
+            def _():
+                last_copy(r, c).wait_send()
+
+            @pl.when(inside(0, -r))
+            def _():
+                last_copy(r, c).wait_recv()
+
+    for c in range(CORES):
+        ref = cat_p.at[core if c == 0 else 1 - core]
+        ref[...] = three(
+            raw_p[c].astype(jnp.float32), lane_half(last_in[0, c]), lane_half(last_in[1, c])
+        )
     begun = 0
     for a in range(TAPS):
         for b in range(TAPS):
             value = correlate(clip_pad, cat_p, a, b)
-            if a > 0:
-                value = value + penalty_weight * correlate(grad_pad, cat_s, a, b)
             for d in range(TAPS):
                 g, t = place(a, b, d)
                 for h in range(2):
                     p = h * GROUPS + g
                     block = tiles(value, h, d)
-                    total[p, :, t] = block + total[p, :, t] if a == 0 else block
+                    total[p, :, t] = block + total[p, :, t]
             done = (a * TAPS + b + 1) * TAPS
             while begun < GROUPS and done >= min((begun + 1) * SHARE, TAPS**3):
                 for h in range(2):
@@ -560,6 +711,7 @@
 def per_device(sizes, clips, weight, bias, head):
     _, frames, _, cols, chans = clips.shape
     count = frames * cols
+    lines = frames * RING
     dp, tm, rows = sizes
     assert (rows, dp * 2, tm // 4, chans) == (RING, RING, DEEP, 2 * LANES)
     dma = pltpu.SemaphoreType.DMA
@@ -569,7 +721,7 @@
     field = pltpu.VMEM((count, chans), jnp.float32)
 
     def pad(n):
-        return pltpu.VMEM((n, 3, cols, chans), jnp.bfloat16)
+        return pltpu.VMEM((n, RING + 2, cols // RING, chans), jnp.bfloat16)
 
     def coded(*lead, units):
         return pltpu.VMEM((*lead, units * SHARE + 1, SUB, LANES), jnp.bfloat16)
@@ -590,10 +742,16 @@
         scratch_shapes=[
             pltpu.VMEM((1, chans), jnp.float32), pltpu.VMEM((1, chans), jnp.float32),
             pltpu.VMEM((TAPS**3, chans, chans), jnp.bfloat16),
+            pltpu.VMEM((frames, cols, chans), jnp.bfloat16),
             pad(2 * frames + 2), pad(frames + 2), pad(2 * frames + 2),
             pltpu.VMEM((TAPS, count, chans), jnp.float32),
             field, field,
-            cat, cat, stage, stage,
+            cat, cat, stage, pltpu.VMEM((count, LANES), jnp.bfloat16),
+            pltpu.VMEM((CORES, count, LANES), jnp.bfloat16),
+            pltpu.VMEM((TAPS, 2, lines, chans), jnp.float32),
+            pltpu.VMEM((TAPS, 2, 3, lines, chans), jnp.float32),
+            pltpu.VMEM((2, lines, chans), jnp.float32),
+            pltpu.VMEM((2, CORES, lines, chans), jnp.float32),
             pltpu.VMEM((PARTS, UNITS, SHARE, SUB, LANES), jnp.float32),
             coded(PARTS, units=8), coded(PARTS, units=8),
             coded(PARTS, units=4), coded(PARTS, units=4),
@@ -602,7 +760,7 @@
             coded(PARTS, CORES, UNITS, units=1),
             pltpu.VMEM((5 * SUB, LANES), jnp.float32),
             pltpu.VMEM((smalls * SUB, LANES), jnp.float32),
-            dma((4,)), *both(24), *both(4), *one(PARTS), *one(PARTS), *one(PARTS), *one(1),
+            dma((4,)), *both(3), *both(24), *both(4), *both(4), *one(PARTS), *one(PARTS), *one(PARTS), *one(1),
             *one(DEEP), *one(PARTS), *one(PARTS), *one(PARTS), *one(2 * PARTS), *one(4),
         ],
         compiler_params=pltpu.CompilerParams(

time: 85.9 us -> 78.9 us (0.919)
  Pallas kernels: 85.1 us -> 77.9 us
    pallas_call x1, Pallas kernels: 82 us -> 74.9 us  [per_device(): pl.pallas_call(functools.partial(kernel, sizes), out_shape=(jax.ShapeDtyp...]
where the time goes in v4:
time: 78.9 us; the launch traced here: 78.6 us
  Pallas kernels  77.9 us (99%)
    pallas_call x1, Pallas kernels, per_device(): pl.pallas_call(functools.partial(kernel, sizes), out_shape=(jax.ShapeDtyp...  74.9 us
    pallas_call x1, Pallas kernels, per_device(): pl.pallas_call(store_kernel, out_shape=(jax.ShapeDtypeStruct((TAPS ** 3,...  3.01 us

profile of v4, /device:TPU:1, one launch (start us, length us, event | category | flops | bytes accessed | tf_op | source)
XLA Modules:
  0.0 78.6 jit_solution(9004871293570146710)
XLA Ops:
  0.6 74.9 %shard_map.67 = (f32[27,32,8,256]{3,2,1,0:T(8,128)S(1)}, f32[1,256]{1,0:T(1,128)S(1)}, f32[1,256]{1,0:T(1,128)S(1)}) custom-call(bf16[2,128,256]{2,1,0:T(8,128)(2,1)} %bitcast.8, bf16[27,256,256]{2,1,0:T(8,128)(2,1)} %bitcast.7, f32[1,256]{1,0:T(1,128)} %bitcast.9, f32[1,256]{1,0:T(1,128)} %bitcast.10), custom_call_target="tpu_custom_call" | custom-call | tf_op jit(solution)/shard_map/pallas_call | solution.py:734
  75.6 3.0 %shard_map.68 = (f32[27,32,8,256]{3,2,1,0:T(8,128)}, f32[1,256]{1,0:T(1,128)}, f32[1,256]{1,0:T(1,128)}) custom-call(f32[27,32,8,256]{3,2,1,0:T(8,128)S(1)} %get-tuple-element.9.grad_ref, f32[1,256]{1,0:T(1,128)S(1)} %get-tuple-element.10.bias_ref, f32[1,256]{1,0:T(1,128)S(1)} %get-tuple-element.11.head_ref), custom_call_target="tpu_custom_call" | custom-call | tf_op jit(solution)/shard_map/pallas_call | solution.py:778

commit v5 on v4

--- a/solution.py
+++ b/solution.py
@@ -20,6 +20,8 @@
 GROUPS = 4
 SHARE = 7
 UNITS = 16
+UNROLL = 4
+WAYS = 2
 PARTS = 2 * GROUPS
 
 
@@ -420,27 +422,38 @@
     routes = []
     for p in range(PARTS):
         first, second = ("x", "y") if p < GROUPS else ("y", "x")
-        m, n = here[first], here[second]
-        if p % 2 == 0:
-            near, bit1, far, bit2 = flip(m), lax.rem((m + 1) // 2, 2), mirror(m), m // 2
-        else:
-            near, bit1, far, bit2 = mirror(m), m // 2, flip(m), lax.rem(m, 2)
-        eight = 8 * bit1
-        four = eight + 4 * bit2
-        routes.append(dict(
-            near=chip(**{first: near}), far=chip(**{first: far}),
-            eight=eight, other8=8 - eight, four=four, other4=2 * eight + 4 - four,
-            unit=four + n, second=second,
-        ))
+        m = here[first]
+        ways = []
+        for v in range(WAYS):
+            if v == 0:
+                near, bit1, far, bit2 = flip(m), lax.rem((m + 1) // 2, 2), mirror(m), m // 2
+            else:
+                near, bit1, far, bit2 = mirror(m), m // 2, flip(m), lax.rem(m, 2)
+            four = 8 * v + 4 * bit1
+            two = four + 2 * bit2
+            ways.append(dict(
+                near=chip(**{first: near}), far=chip(**{first: far}),
+                four=four, other4=16 * v + 4 - four, two=two, other2=2 * four + 2 - two,
+            ))
+        routes.append(dict(ways=ways, second=second))
+
+    def unit_of(p, n):
+        low, high = (way["two"] for way in routes[p]["ways"])
+        upper = n // 2
+        return (1 - upper) * (low + n) + upper * (high + n - 2)
+
+    for p, route in enumerate(routes):
+        route["unit"] = unit_of(p, here[route["second"]])
 
     def encode(p, base, units, code, at):
-        def peak(k, top):
+        def peak(k, tops):
             for t in range(SHARE):
-                top = jnp.maximum(top, jnp.abs(total[p, base + k, t]))
-            return top
-
-        zero = jnp.zeros((SUB, LANES), jnp.float32)
-        top = peak(0, zero) if units == 1 else lax.fori_loop(0, units, peak, zero)
+                tops = jnp.maximum(tops, jnp.abs(total[p, base + k, t]))
+            return tops
+
+        top = lax.fori_loop(
+            0, units, peak, jnp.zeros((SUB, LANES), jnp.float32), unroll=min(units, UNROLL)
+        )
         top = (top * 1.01 + 1e-30).astype(jnp.bfloat16)
         rate = SPAN / top.astype(jnp.float32)
         code[(*at, units * SHARE)] = top
@@ -451,10 +464,7 @@
             ).astype(jnp.bfloat16)
             return carry
 
-        if units == 1:
-            fill(0, 0)
-        else:
-            lax.fori_loop(0, units, fill, 0)
+        lax.fori_loop(0, units, fill, 0, unroll=min(units, UNROLL))
 
     def absorb(p, base, units, lands):
         scales = [
@@ -470,16 +480,15 @@
             total[p, base + k] = value
             return carry
 
-        if units == 1:
-            add(0, 0)
-        else:
-            lax.fori_loop(0, units, add, 0)
-
-    def copy1(p):
-        return send(code1.at[p], land1.at[p], send1.at[0], recv1.at[p], routes[p]["near"])
-
-    def copy2(p):
-        return send(code2.at[p], land2.at[p], send2.at[0], recv2.at[p], routes[p]["far"])
+        lax.fori_loop(0, units, add, 0, unroll=min(units, UNROLL))
+
+    def halving(p, v, code, land, send_sem, recv_sem, to):
+        return send(
+            code.at[p, v], land.at[p, v], send_sem.at[0], recv_sem.at[p], routes[p]["ways"][v][to]
+        )
+
+    def arrived(block, recv_sem, slot):
+        send(block, block, send1.at[0], recv_sem.at[slot], partner).wait_recv()
 
     def copy3(p):
         second = routes[p]["second"]
@@ -492,17 +501,19 @@
         ]
 
     def start1(p):
-        encode(p, routes[p]["other8"], 8, code1, (p,))
-        copy1(p).start()
+        for v, way in enumerate(routes[p]["ways"]):
+            encode(p, way["other4"], 4, code1, (p, v))
+            halving(p, v, code1, land1, send1, recv1, "near").start()
 
     def start2(p):
-        encode(p, routes[p]["other4"], 4, code2, (p,))
-        copy2(p).start()
+        for v, way in enumerate(routes[p]["ways"]):
+            encode(p, way["other2"], 2, code2, (p, v))
+            halving(p, v, code2, land2, send2, recv2, "far").start()
 
     def start3(p):
         second = routes[p]["second"]
         for k, (copy, other) in enumerate(zip(copy3(p), ring_peers(second, RING))):
-            encode(p, routes[p]["four"] + other, 1, code3, (p, k))
+            encode(p, unit_of(p, other), 1, code3, (p, k))
             copy.start()
 
     def correlate(pad, cat, a, b):
@@ -568,14 +579,16 @@
     small_start(1)
     order = [h * GROUPS + g for g in range(GROUPS) for h in range(2)]
     for p in order:
-        copy1(p).wait_recv()
-        absorb(p, routes[p]["eight"], 8, [(land1, (p,))])
+        arrived(land1.at[p], recv1, p)
+        for v, way in enumerate(routes[p]["ways"]):
+            absorb(p, way["four"], 4, [(land1, (p, v))])
         start2(p)
     small_end(1)
     small_start(2)
     for p in order:
-        copy2(p).wait_recv()
-        absorb(p, routes[p]["four"], 4, [(land2, (p,))])
+        arrived(land2.at[p], recv2, p)
+        for v, way in enumerate(routes[p]["ways"]):
+            absorb(p, way["two"], 2, [(land2, (p, v))])
         start3(p)
     small_end(2)
     small_start(3)
@@ -624,19 +637,21 @@
             for k, other in enumerate(ring_peers(second, RING))
         ]
 
-    def far_copy(p):
-        block = full.at[p, core, pl.ds(routes[p]["four"], 4)]
-        return send(block, block, far_send.at[0], far_recv.at[p], routes[p]["far"])
-
-    def near_copy(p):
-        block = full.at[p, core, pl.ds(routes[p]["eight"], 8)]
-        return send(block, block, near_send.at[0], near_recv.at[p], routes[p]["near"])
-
-    def core_copy(p, second):
-        base = routes[p]["other8"] if second else routes[p]["eight"]
-        block = full.at[p, core, pl.ds(base, 8)]
-        slot = 2 * p + second
-        return send(block, block, core_send.at[0], core_recv.at[slot], partner)
+    def far_copy(p, v):
+        block = full.at[p, core, pl.ds(routes[p]["ways"][v]["two"], 2)]
+        return send(block, block, far_send.at[0], far_recv.at[p], routes[p]["ways"][v]["far"])
+
+    def near_copy(p, v):
+        block = full.at[p, core, pl.ds(routes[p]["ways"][v]["four"], 4)]
+        return send(block, block, near_send.at[0], near_recv.at[p], routes[p]["ways"][v]["near"])
+
+    def core_start(p, second):
+        for way in routes[p]["ways"]:
+            block = full.at[p, core, pl.ds(way["other4"] if second else way["four"], 4)]
+            send(block, block, core_send.at[0], core_recv.at[2 * p + second], partner).start()
+
+    def units(count):
+        return full.at[0, 0, pl.ds(0, count)]
 
     for p in order:
         @pl.when(z != p)
@@ -648,13 +663,14 @@
     for p in order:
         three = full.at[p, core, pl.ds(0, RING - 1)]
         send(three, three, qsend.at[0], qrecv.at[p], partner).wait_recv()
-        far_copy(p).start()
-    def reveal(p, c, base):
+        for v in range(WAYS):
+            far_copy(p, v).start()
+    def reveal(p, c, which):
         h, g = p // GROUPS, p % GROUPS
         taps = min(SHARE, TAPS**3 - g * SHARE)
         lane = pl.ds(pl.multiple_of(c * LANES, LANES), LANES)
 
-        def one(k, carry):
+        def one(base, k, carry):
             scale = full[p, c, base + k, SHARE].astype(jnp.float32) * (1.0 / (SPAN * math.log(2.0)))
             block = full[p, c, base + k, pl.ds(0, taps)].astype(jnp.float32)
             out_ref[pl.ds(g * SHARE, taps), h * UNITS + base + k, :, lane] = (
@@ -662,27 +678,36 @@
             )
             return carry
 
-        lax.fori_loop(0, 8, one, 0)
+        for way in routes[p]["ways"]:
+            lax.fori_loop(0, 4, functools.partial(one, way[which]), 0, unroll=UNROLL)
 
     for k, ref in enumerate((bias_out, head_out)):
         at = (len(small_targets)) * SUB + 2 * k
         ref[:, pl.ds(0, LANES)] = small_mine[pl.ds(at, 1)]
         ref[:, pl.ds(LANES, LANES)] = small_mine[pl.ds(at + 1, 1)]
     for p in order:
-        far_copy(p).wait_recv()
-        near_copy(p).start()
-        core_copy(p, 0).start()
+        arrived(units(4), far_recv, p)
+        for v in range(WAYS):
+            near_copy(p, v).start()
+        core_start(p, 0)
+    def reveal_far(p):
+        arrived(units(8), core_recv, 2 * p)
+        reveal(p, 1 - core, "four")
+
+    for k, p in enumerate(order):
+        reveal(p, core, "four")
+        if k >= 2:
+            reveal_far(order[k - 2])
+        arrived(units(8), near_recv, p)
+        core_start(p, 1)
+        if k >= 1:
+            reveal(order[k - 1], core, "other4")
+    for p in order[-2:]:
+        reveal_far(p)
+    reveal(order[-1], core, "other4")
     for p in order:
-        reveal(p, core, routes[p]["eight"])
-        near_copy(p).wait_recv()
-        core_copy(p, 1).start()
-    for p in order:
-        reveal(p, core, routes[p]["other8"])
-        core_copy(p, 0).wait_recv()
-        reveal(p, 1 - core, routes[p]["eight"])
-    for p in order:
-        core_copy(p, 1).wait_recv()
-        reveal(p, 1 - core, routes[p]["other8"])
+        arrived(units(8), core_recv, 2 * p + 1)
+        reveal(p, 1 - core, "other4")
     for block, sem in (
         (small_land, small_send), (code1, send1), (code2, send2), (code3, send3),
         (code4.at[pl.ds(0, DEEP - 1)], send4), (full.at[0, 0, pl.ds(0, DEEP - 1)], zsend),
@@ -753,8 +778,8 @@
             pltpu.VMEM((2, lines, chans), jnp.float32),
             pltpu.VMEM((2, CORES, lines, chans), jnp.float32),
             pltpu.VMEM((PARTS, UNITS, SHARE, SUB, LANES), jnp.float32),
-            coded(PARTS, units=8), coded(PARTS, units=8),
-            coded(PARTS, units=4), coded(PARTS, units=4),
+            coded(PARTS, WAYS, units=4), coded(PARTS, WAYS, units=4),
+            coded(PARTS, WAYS, units=2), coded(PARTS, WAYS, units=2),
             coded(PARTS, RING - 1, units=1), coded(PARTS, RING - 1, units=1),
             coded(DEEP, units=1), coded(DEEP, units=1),
             coded(PARTS, CORES, UNITS, units=1),

time: 78.9 us -> 76.8 us (0.973)
  Pallas kernels: 77.9 us -> 76.1 us
    pallas_call x1, Pallas kernels: 74.9 us -> 73.1 us  [per_device(): pl.pallas_call(functools.partial(kernel, sizes), out_shape=(jax.ShapeDtyp...]
where the time goes in v5:
time: 76.8 us; the launch traced here: 76.7 us
  Pallas kernels  76.1 us (99%)
    pallas_call x1, Pallas kernels, per_device(): pl.pallas_call(functools.partial(kernel, sizes), out_shape=(jax.ShapeDtyp...  73.1 us
    pallas_call x1, Pallas kernels, per_device(): pl.pallas_call(store_kernel, out_shape=(jax.ShapeDtypeStruct((TAPS ** 3,...  3.01 us

profile of v5, /device:TPU:1, one launch (start us, length us, event | category | flops | bytes accessed | tf_op | source)
XLA Modules:
  0.0 76.7 jit_solution(17297966474771188777)
XLA Ops:
  0.6 73.1 %shard_map.67 = (f32[27,32,8,256]{3,2,1,0:T(8,128)S(1)}, f32[1,256]{1,0:T(1,128)S(1)}, f32[1,256]{1,0:T(1,128)S(1)}) custom-call(bf16[2,128,256]{2,1,0:T(8,128)(2,1)} %bitcast.8, bf16[27,256,256]{2,1,0:T(8,128)(2,1)} %bitcast.7, f32[1,256]{1,0:T(1,128)} %bitcast.9, f32[1,256]{1,0:T(1,128)} %bitcast.10), custom_call_target="tpu_custom_call" | custom-call | tf_op jit(solution)/shard_map/pallas_call | solution.py:759
  73.7 3.0 %shard_map.68 = (f32[27,32,8,256]{3,2,1,0:T(8,128)}, f32[1,256]{1,0:T(1,128)}, f32[1,256]{1,0:T(1,128)}) custom-call(f32[27,32,8,256]{3,2,1,0:T(8,128)S(1)} %get-tuple-element.9.grad_ref, f32[1,256]{1,0:T(1,128)S(1)} %get-tuple-element.10.bias_ref, f32[1,256]{1,0:T(1,128)S(1)} %get-tuple-element.11.head_ref), custom_call_target="tpu_custom_call" | custom-call | tf_op jit(solution)/shard_map/pallas_call | solution.py:803

commit v6 on v5

--- a/solution.py
+++ b/solution.py
@@ -37,7 +37,7 @@
     sizes, clips_ref, weight_ref, bias_hbm, head_hbm,
     out_ref, bias_out, head_out,
     bias_ref, head_ref, w_ref, clips_vm, clip_pad, score_pad, grad_pad, acc, slope_ref, curve_ref,
-    cat_s, cat_p, stage_s, stage_p, raw_p, edge_out, edge_in, last_out, last_in, total,
+    cat_s, cat_p, stage_s, stage_p, raw_p, side_out, side_in, edge_out, edge_in, last_out, last_in, total,
     code1, land1, code2, land2, code3, land3, code4, land4, full, small_mine, small_land,
     local_sem, turn_send, turn_recv, halo_send, halo_recv, last_send, last_recv,
     pair_send, pair_recv, send1, recv1, send2, recv2,
@@ -91,6 +91,7 @@
         for at in (base, base + frames + 1):
             pad[at, pl.ds(1, RING)] = jnp.zeros((RING, cols, chans), pad.dtype)
     edge_in[...] = jnp.zeros_like(edge_in)
+    side_in[...] = jnp.zeros_like(side_in)
     last_in[...] = jnp.zeros_like(last_in)
 
     moves = [(t, r) for t in (-1, 0, 1) for r in (-1, 0, 1) if (t, r) != (0, 0)]
@@ -141,14 +142,35 @@
             device(tm=me["tm"] + t, rows=other),
         )
 
+    def side_copy(t, step):
+        other = lax.rem(me["rows"] + step, RING)
+        return send(
+            side_out.at[other], side_in.at[1 - t, me["rows"]],
+            turn_send.at[4 + t], turn_recv.at[4 + t],
+            device(tm=me["tm"] + t, rows=other),
+        )
+
     def turn_start():
         for step in range(1, RING):
             turn_copy(0, step).start()
+        for other in range(RING):
+            at = other * cols
+            lines_out = [
+                clips_vm[f, c : c + 1].astype(jnp.float32) if 0 <= c < wide
+                else jnp.zeros((1, chans), jnp.float32)
+                for c in (at - 1, at + cols) for f in range(frames)
+            ]
+            lines_out.append(jnp.zeros((SUB - 2 * frames, chans), jnp.float32))
+            side_out[other] = jnp.concatenate(lines_out, axis=0).astype(jnp.bfloat16)
+        for step in range(1, RING):
+            side_copy(0, step).start()
         for t in (-1, 1):
             @pl.when(inside(t, 0))
             def _():
                 for step in range(RING):
                     turn_copy(t, step).start()
+                    side_copy(t, step).start()
+        side_in[1, me["rows"]] = side_out[me["rows"]]
 
     def turn_wait(level):
         if level:
@@ -157,25 +179,48 @@
             copy.wait_recv()
             copy.wait_send()
             return
+        block = side_in.at[1, pl.ds(0, RING - 1)]
+        copy = send(block, block, turn_send.at[4], turn_recv.at[4], partner)
+        copy.wait_recv()
+        copy.wait_send()
         for t in (-1, 1):
-            block = clip_pad.at[shift, pl.ds(1, RING)]
-            copy = send(block, block, turn_send.at[1 + t], turn_recv.at[1 + t], partner)
+            block, side = clip_pad.at[shift, pl.ds(1, RING)], side_in.at[0]
+            copies = [
+                send(block, block, turn_send.at[1 + t], turn_recv.at[1 + t], partner),
+                send(side, side, turn_send.at[4 + t], turn_recv.at[4 + t], partner),
+            ]
 
             @pl.when(inside(t, 0))
             def _():
-                copy.wait_send()
+                for copy in copies:
+                    copy.wait_send()
 
             @pl.when(inside(-t, 0))
             def _():
-                copy.wait_recv()
+                for copy in copies:
+                    copy.wait_recv()
+
+        line = lax.broadcasted_iota(jnp.int32, (lines, chans), 0)
+        for k in range(3):
+            blocks = [side_in[k, r].astype(jnp.float32) for r in range(RING)]
+            for side in range(2):
+                value = jnp.zeros((lines, chans), jnp.float32)
+                for r in range(RING):
+                    for f in range(frames):
+                        at = side * frames + f
+                        value = jnp.where(
+                            line == f * RING + r,
+                            jnp.broadcast_to(blocks[r][at : at + 1], (lines, chans)), value,
+                        )
+                edge_in[0, side, k] = value
 
     def halo_copy(which, pad, t, r):
-        slot = which * len(moves) + moves.index((t, r))
+        slot = (which - 1) * len(moves) + moves.index((t, r))
         target = device(tm=me["tm"] + t, rows=me["rows"] + r)
         sems = halo_send.at[slot], halo_recv.at[slot]
         if r != 0:
             side = 0 if r > 0 else 1
-            return send(edge_out.at[which, side], edge_in.at[which, side, 1 - t], *sems, target)
+            return send(edge_out.at[which - 1, side], edge_in.at[which, side, 1 - t], *sems, target)
         pair = pad.shape[0] > frames + 2
         mine, base = (shift, 2 - shift) if pair else (0, 0)
         src = mine + frames if t > 0 else mine + 1
@@ -188,22 +233,16 @@
         block = value.reshape(lines, cols, value.shape[-1])
         return block[:, cols - 1], block[:, 0]
 
-    def halo_start(which, pad, value, skip=False):
+    def halo_start(which, pad, value):
         for side, rows_out in enumerate(edge_rows(value)):
-            edge_out[which, side] = rows_out
+            edge_out[which - 1, side] = rows_out
         for t, r in sorted(moves, key=lambda move: move[1] != 0):
-            if skip and r == 0:
-                continue
-
             @pl.when(inside(t, r))
             def _():
                 halo_copy(which, pad, t, r).start()
 
-    def halo_wait(which, pad, skip=False):
+    def halo_wait(which, pad):
         for t, r in moves:
-            if skip and r == 0:
-                continue
-
             @pl.when(inside(t, r))
             def _():
                 halo_copy(which, pad, t, r).wait_send()
@@ -323,14 +362,7 @@
     head_copy.wait()
     pair_clips, pair_grads = pair_frames(clip_pad, 0), pair_frames(grad_pad, 1)
     turn_wait(True)
-    clips = clip_pad[pl.ds(shift + 1, frames), pl.ds(1, RING)].reshape(count, chans)
-    halo_start(0, clip_pad, clips.astype(jnp.float32), True)
-
-    def wait_clips():
-        turn_wait(False)
-        halo_wait(0, clip_pad, True)
-
-    pre = conv(0, clip_pad, False, wait_clips, pair_clips.start) + bias_ref[...]
+    pre = conv(0, clip_pad, False, lambda: turn_wait(False), pair_clips.start) + bias_ref[...]
     sig = jax.nn.sigmoid(pre)
     slope = sig * (1.0 + pre * (1.0 - sig))
     slope_ref[...] = slope
@@ -773,7 +805,9 @@
             field, field,
             cat, cat, stage, pltpu.VMEM((count, LANES), jnp.bfloat16),
             pltpu.VMEM((CORES, count, LANES), jnp.bfloat16),
-            pltpu.VMEM((TAPS, 2, lines, chans), jnp.float32),
+            pltpu.VMEM((RING, SUB, chans), jnp.bfloat16),
+            pltpu.VMEM((3, RING, SUB, chans), jnp.bfloat16),
+            pltpu.VMEM((2, 2, lines, chans), jnp.float32),
             pltpu.VMEM((TAPS, 2, 3, lines, chans), jnp.float32),
             pltpu.VMEM((2, lines, chans), jnp.float32),
             pltpu.VMEM((2, CORES, lines, chans), jnp.float32),
@@ -785,7 +819,7 @@
             coded(PARTS, CORES, UNITS, units=1),
             pltpu.VMEM((5 * SUB, LANES), jnp.float32),
             pltpu.VMEM((smalls * SUB, LANES), jnp.float32),
-            dma((4,)), *both(3), *both(24), *both(4), *both(4), *one(PARTS), *one(PARTS), *one(PARTS), *one(1),
+            dma((4,)), *both(6), *both(16), *both(4), *both(4), *one(PARTS), *one(PARTS), *one(PARTS), *one(1),
             *one(DEEP), *one(PARTS), *one(PARTS), *one(PARTS), *one(2 * PARTS), *one(4),
         ],
         compiler_params=pltpu.CompilerParams(

time: 76.8 us -> 75 us (0.977)
  Pallas kernels: 76.1 us -> 74.3 us
    pallas_call x1, Pallas kernels: 73.1 us -> 71.3 us  [per_device(): pl.pallas_call(functools.partial(kernel, sizes), out_shape=(jax.ShapeDtyp...]
where the time goes in v6:
time: 75 us; the launch traced here: 74.9 us
  Pallas kernels  74.3 us (99%)
    pallas_call x1, Pallas kernels, per_device(): pl.pallas_call(functools.partial(kernel, sizes), out_shape=(jax.ShapeDtyp...  71.3 us
    pallas_call x1, Pallas kernels, per_device(): pl.pallas_call(store_kernel, out_shape=(jax.ShapeDtypeStruct((TAPS ** 3,...  3.01 us

profile of v6, /device:TPU:1, one launch (start us, length us, event | category | flops | bytes accessed | tf_op | source)
XLA Modules:
  0.0 74.9 jit_solution(18092305638580131923)
XLA Ops:
  0.6 71.3 %shard_map.67 = (f32[27,32,8,256]{3,2,1,0:T(8,128)S(1)}, f32[1,256]{1,0:T(1,128)S(1)}, f32[1,256]{1,0:T(1,128)S(1)}) custom-call(bf16[2,128,256]{2,1,0:T(8,128)(2,1)} %bitcast.8, bf16[27,256,256]{2,1,0:T(8,128)(2,1)} %bitcast.7, f32[1,256]{1,0:T(1,128)} %bitcast.9, f32[1,256]{1,0:T(1,128)} %bitcast.10), custom_call_target="tpu_custom_call" | custom-call | tf_op jit(solution)/shard_map/pallas_call | solution.py:791
  71.9 3.0 %shard_map.68 = (f32[27,32,8,256]{3,2,1,0:T(8,128)}, f32[1,256]{1,0:T(1,128)}, f32[1,256]{1,0:T(1,128)}) custom-call(f32[27,32,8,256]{3,2,1,0:T(8,128)S(1)} %get-tuple-element.9.grad_ref, f32[1,256]{1,0:T(1,128)S(1)} %get-tuple-element.10.bias_ref, f32[1,256]{1,0:T(1,128)S(1)} %get-tuple-element.11.head_ref), custom_call_target="tpu_custom_call" | custom-call | tf_op jit(solution)/shard_map/pallas_call | solution.py:837

commit v7 on v6

--- a/solution.py
+++ b/solution.py
@@ -234,12 +234,17 @@
         return block[:, cols - 1], block[:, 0]
 
     def halo_start(which, pad, value):
-        for side, rows_out in enumerate(edge_rows(value)):
-            edge_out[which - 1, side] = rows_out
-        for t, r in sorted(moves, key=lambda move: move[1] != 0):
-            @pl.when(inside(t, r))
-            def _():
-                halo_copy(which, pad, t, r).start()
+        for level in (True, False):
+            if not level:
+                for side, rows_out in enumerate(edge_rows(value)):
+                    edge_out[which - 1, side] = rows_out
+            for t, r in moves:
+                if (r == 0) != level:
+                    continue
+
+                @pl.when(inside(t, r))
+                def _():
+                    halo_copy(which, pad, t, r).start()
 
     def halo_wait(which, pad):
         for t, r in moves:
@@ -395,17 +400,11 @@
     value = pre_grad.astype(jnp.bfloat16).astype(jnp.float32)
     for side, rows_out in enumerate(edge_rows(value)):
         last_out[side] = rows_out
-    stage_p[...] = lane_half(value, False).astype(jnp.bfloat16)
-    pair_p = send(stage_p, raw_p.at[1], pair_send.at[3], pair_recv.at[3], partner)
-    pair_p.start()
-    raw_p[0] = lane_half(value).astype(jnp.bfloat16)
-
     def last_copy(r, c):
         side = 0 if r > 0 else 1
-        slot = 2 * side + c
         other = core if c == 0 else 1 - core
         return send(
-            last_out.at[side], last_in.at[side, c], last_send.at[slot], last_recv.at[slot],
+            last_out.at[side], last_in.at[side, c], last_send.at[side], last_recv.at[side],
             device(tm=me["tm"] - core + other, rows=me["rows"] + r),
         )
 
@@ -414,6 +413,11 @@
         def _():
             for c in range(CORES):
                 last_copy(r, c).start()
+
+    stage_p[...] = lane_half(value, False).astype(jnp.bfloat16)
+    pair_p = send(stage_p, raw_p.at[core], pair_send.at[3], pair_recv.at[3], partner)
+    pair_p.start()
+    raw_p[core] = lane_half(value).astype(jnp.bfloat16)
 
     small_mine[...] = jnp.zeros_like(small_mine)
     for k, value in enumerate((pre_grad, back * slope_ref[...])):
@@ -516,7 +520,7 @@
 
     def halving(p, v, code, land, send_sem, recv_sem, to):
         return send(
-            code.at[p, v], land.at[p, v], send_sem.at[0], recv_sem.at[p], routes[p]["ways"][v][to]
+            code.at[p, v], land.at[p, v], send_sem.at[0], recv_sem.at[p % GROUPS], routes[p]["ways"][v][to]
         )
 
     def arrived(block, recv_sem, slot):
@@ -526,7 +530,7 @@
         second = routes[p]["second"]
         return [
             send(
-                code3.at[p, k], land3.at[p, k], send3.at[0], recv3.at[p],
+                code3.at[p, k], land3.at[p, k], send3.at[0], recv3.at[p % GROUPS],
                 chip(**{second: other}),
             )
             for k, other in enumerate(ring_peers(second, RING))
@@ -550,7 +554,7 @@
 
     def correlate(pad, cat, a, b):
         left = pad[a : a + 2 * frames, b : b + RING].reshape(2 * count, chans)
-        right = cat[...].reshape(2 * count, TAPS * LANES)
+        right = cat[...].reshape(2 * count, cat.shape[-1])
         return lax.dot_general(
             left, right, (((0,), (0,)), ((), ())), preferred_element_type=jnp.float32
         )
@@ -568,38 +572,52 @@
     pair_s.wait()
     pair_grads.wait()
     for a in range(TAPS):
+        if a == 1:
+            pair_clips.wait()
+            pair_p.wait()
         for b in range(TAPS):
             value = penalty_weight * correlate(grad_pad, cat_s, a, b)
+            level = correlate(clip_pad, raw_p, a, b) if a > 0 else None
             for d in range(TAPS):
                 g, t = place(a, b, d)
                 for h in range(2):
-                    total[h * GROUPS + g, :, t] = tiles(value, h, d)
-    pair_clips.wait()
-    pair_p.wait()
+                    block = tiles(value, h, d)
+                    if a > 0 and d == 1:
+                        block = block + tiles(level, h, 0)
+                    total[h * GROUPS + g, :, t] = block
+    for b in range(TAPS):
+        level = correlate(clip_pad, raw_p, 0, b)
+        g, t = place(0, b, 1)
+        for h in range(2):
+            total[h * GROUPS + g, :, t] = total[h * GROUPS + g, :, t] + tiles(level, h, 0)
     for r in (-1, 1):
-        for c in range(CORES):
-            @pl.when(inside(0, r))
-            def _():
-                last_copy(r, c).wait_send()
-
-            @pl.when(inside(0, -r))
-            def _():
-                last_copy(r, c).wait_recv()
+        side = 0 if r > 0 else 1
+        both = last_in.at[side]
+        copy = send(both, both, last_send.at[side], last_recv.at[side], partner)
+
+        @pl.when(inside(0, r))
+        def _():
+            copy.wait_send()
+
+        @pl.when(inside(0, -r))
+        def _():
+            copy.wait_recv()
 
     for c in range(CORES):
-        ref = cat_p.at[core if c == 0 else 1 - core]
-        ref[...] = three(
-            raw_p[c].astype(jnp.float32), lane_half(last_in[0, c]), lane_half(last_in[1, c])
-        )
+        at = core if c == 0 else 1 - core
+        value = raw_p[at].astype(jnp.float32)
+        cat_p[at] = jnp.concatenate([
+            later(value, lane_half(last_in[1, c])), earlier(value, lane_half(last_in[0, c]))
+        ], axis=1).astype(jnp.bfloat16)
     begun = 0
     for a in range(TAPS):
         for b in range(TAPS):
             value = correlate(clip_pad, cat_p, a, b)
-            for d in range(TAPS):
+            for d in (0, 2):
                 g, t = place(a, b, d)
                 for h in range(2):
                     p = h * GROUPS + g
-                    block = tiles(value, h, d)
+                    block = tiles(value, h, d // 2)
                     total[p, :, t] = block + total[p, :, t]
             done = (a * TAPS + b + 1) * TAPS
             while begun < GROUPS and done >= min((begun + 1) * SHARE, TAPS**3):
@@ -611,14 +629,16 @@
     small_start(1)
     order = [h * GROUPS + g for g in range(GROUPS) for h in range(2)]
     for p in order:
-        arrived(land1.at[p], recv1, p)
+        if p < GROUPS:
+            arrived(land1.at[pl.ds(0, 2)], recv1, p)
         for v, way in enumerate(routes[p]["ways"]):
             absorb(p, way["four"], 4, [(land1, (p, v))])
         start2(p)
     small_end(1)
     small_start(2)
     for p in order:
-        arrived(land2.at[p], recv2, p)
+        if p < GROUPS:
+            arrived(land2.at[pl.ds(0, 2)], recv2, p)
         for v, way in enumerate(routes[p]["ways"]):
             absorb(p, way["two"], 2, [(land2, (p, v))])
         start3(p)
@@ -631,7 +651,8 @@
         return send(code4.at[p], land4.at[z], send4.at[0], recv4.at[0], chip(z=p))
 
     for p in order:
-        send(land3.at[p], land3.at[p], send3.at[0], recv3.at[p], partner).wait_recv()
+        if p < GROUPS:
+            arrived(land3.at[pl.ds(0, 2)], recv3, p)
         absorb(p, routes[p]["unit"], 1, [(land3, (p, k)) for k in range(RING - 1)])
 
         @pl.when(z != p)
@@ -665,22 +686,22 @@
         second = routes[p]["second"]
         block = full.at[p, core, routes[p]["unit"]]
         return [
-            send(block, block, qsend.at[0], qrecv.at[p], chip(**{second: other}))
+            send(block, block, qsend.at[0], qrecv.at[p % GROUPS], chip(**{second: other}))
             for k, other in enumerate(ring_peers(second, RING))
         ]
 
     def far_copy(p, v):
         block = full.at[p, core, pl.ds(routes[p]["ways"][v]["two"], 2)]
-        return send(block, block, far_send.at[0], far_recv.at[p], routes[p]["ways"][v]["far"])
+        return send(block, block, far_send.at[0], far_recv.at[p % GROUPS], routes[p]["ways"][v]["far"])
 
     def near_copy(p, v):
         block = full.at[p, core, pl.ds(routes[p]["ways"][v]["four"], 4)]
-        return send(block, block, near_send.at[0], near_recv.at[p], routes[p]["ways"][v]["near"])
+        return send(block, block, near_send.at[0], near_recv.at[p % GROUPS], routes[p]["ways"][v]["near"])
 
     def core_start(p, second):
         for way in routes[p]["ways"]:
             block = full.at[p, core, pl.ds(way["other4"] if second else way["four"], 4)]
-            send(block, block, core_send.at[0], core_recv.at[2 * p + second], partner).start()
+            send(block, block, core_send.at[0], core_recv.at[2 * (p % GROUPS) + second], partner).start()
 
     def units(count):
         return full.at[0, 0, pl.ds(0, count)]
@@ -693,8 +714,8 @@
         for copy in qcopies(p):
             copy.start()
     for p in order:
-        three = full.at[p, core, pl.ds(0, RING - 1)]
-        send(three, three, qsend.at[0], qrecv.at[p], partner).wait_recv()
+        if p < GROUPS:
+            arrived(units(2 * (RING - 1)), qrecv, p)
         for v in range(WAYS):
             far_copy(p, v).start()
     def reveal(p, c, which):
@@ -717,29 +738,32 @@
         at = (len(small_targets)) * SUB + 2 * k
         ref[:, pl.ds(0, LANES)] = small_mine[pl.ds(at, 1)]
         ref[:, pl.ds(LANES, LANES)] = small_mine[pl.ds(at + 1, 1)]
-    for p in order:
-        arrived(units(4), far_recv, p)
+    def reveal_core(p, second):
+        if p < GROUPS:
+            arrived(units(16), core_recv, 2 * p + second)
+        reveal(p, 1 - core, "other4" if second else "four")
+
+    for k, p in enumerate(order):
+        if p < GROUPS:
+            arrived(units(8), far_recv, p)
         for v in range(WAYS):
             near_copy(p, v).start()
         core_start(p, 0)
-    def reveal_far(p):
-        arrived(units(8), core_recv, 2 * p)
-        reveal(p, 1 - core, "four")
-
+        if k >= 1:
+            reveal(order[k - 1], core, "four")
+    reveal(order[-1], core, "four")
     for k, p in enumerate(order):
-        reveal(p, core, "four")
-        if k >= 2:
-            reveal_far(order[k - 2])
-        arrived(units(8), near_recv, p)
+        reveal_core(p, 0)
+        if p < GROUPS:
+            arrived(units(16), near_recv, p)
         core_start(p, 1)
         if k >= 1:
             reveal(order[k - 1], core, "other4")
-    for p in order[-2:]:
-        reveal_far(p)
+        if k >= 4:
+            reveal_core(order[k - 4], 1)
     reveal(order[-1], core, "other4")
-    for p in order:
-        arrived(units(8), core_recv, 2 * p + 1)
-        reveal(p, 1 - core, "other4")
+    for p in order[-4:]:
+        reveal_core(p, 1)
     for block, sem in (
         (small_land, small_send), (code1, send1), (code2, send2), (code3, send3),
         (code4.at[pl.ds(0, DEEP - 1)], send4), (full.at[0, 0, pl.ds(0, DEEP - 1)], zsend),
@@ -803,7 +827,7 @@
             pad(2 * frames + 2), pad(frames + 2), pad(2 * frames + 2),
             pltpu.VMEM((TAPS, count, chans), jnp.float32),
             field, field,
-            cat, cat, stage, pltpu.VMEM((count, LANES), jnp.bfloat16),
+            cat, pltpu.VMEM((CORES, count, 2 * LANES), jnp.bfloat16), stage, pltpu.VMEM((count, LANES), jnp.bfloat16),
             pltpu.VMEM((CORES, count, LANES), jnp.bfloat16),
             pltpu.VMEM((RING, SUB, chans), jnp.bfloat16),
             pltpu.VMEM((3, RING, SUB, chans), jnp.bfloat16),
@@ -819,8 +843,9 @@
             coded(PARTS, CORES, UNITS, units=1),
             pltpu.VMEM((5 * SUB, LANES), jnp.float32),
             pltpu.VMEM((smalls * SUB, LANES), jnp.float32),
-            dma((4,)), *both(6), *both(16), *both(4), *both(4), *one(PARTS), *one(PARTS), *one(PARTS), *one(1),
-            *one(DEEP), *one(PARTS), *one(PARTS), *one(PARTS), *one(2 * PARTS), *one(4),
+            dma((4,)), *both(6), *both(16), *both(2), *both(4),
+            *one(GROUPS), *one(GROUPS), *one(GROUPS), *one(1),
+            *one(DEEP), *one(GROUPS), *one(GROUPS), *one(GROUPS), *one(2 * GROUPS), *one(4),
         ],
         compiler_params=pltpu.CompilerParams(
             collective_id=0, has_side_effects=True, vmem_limit_bytes=40 * 1024 * 1024

time: 75 us -> 74.9 us (level)
  no operation moved by 1% of the time
where the time goes in v7:
time: 74.9 us; the launch traced here: 74.8 us
  Pallas kernels  74.2 us (99%)
    pallas_call x1, Pallas kernels, per_device(): pl.pallas_call(functools.partial(kernel, sizes), out_shape=(jax.ShapeDtyp...  71.2 us
    pallas_call x1, Pallas kernels, per_device(): pl.pallas_call(store_kernel, out_shape=(jax.ShapeDtypeStruct((TAPS ** 3,...  3.01 us

profile of v7, /device:TPU:1, one launch (start us, length us, event | category | flops | bytes accessed | tf_op | source)
XLA Modules:
  0.0 74.8 jit_solution(9944787538476118107)
XLA Ops:
  0.6 71.2 %shard_map.67 = (f32[27,32,8,256]{3,2,1,0:T(8,128)S(1)}, f32[1,256]{1,0:T(1,128)S(1)}, f32[1,256]{1,0:T(1,128)S(1)}) custom-call(bf16[2,128,256]{2,1,0:T(8,128)(2,1)} %bitcast.8, bf16[27,256,256]{2,1,0:T(8,128)(2,1)} %bitcast.7, f32[1,256]{1,0:T(1,128)} %bitcast.9, f32[1,256]{1,0:T(1,128)} %bitcast.10), custom_call_target="tpu_custom_call" | custom-call | tf_op jit(solution)/shard_map/pallas_call | solution.py:815
  71.8 3.0 %shard_map.68 = (f32[27,32,8,256]{3,2,1,0:T(8,128)}, f32[1,256]{1,0:T(1,128)}, f32[1,256]{1,0:T(1,128)}) custom-call(f32[27,32,8,256]{3,2,1,0:T(8,128)S(1)} %get-tuple-element.9.grad_ref, f32[1,256]{1,0:T(1,128)S(1)} %get-tuple-element.10.bias_ref, f32[1,256]{1,0:T(1,128)S(1)} %get-tuple-element.11.head_ref), custom_call_target="tpu_custom_call" | custom-call | tf_op jit(solution)/shard_map/pallas_call | solution.py:862

commit v8 on v7

--- a/solution.py
+++ b/solution.py
@@ -520,7 +520,7 @@
 
     def halving(p, v, code, land, send_sem, recv_sem, to):
         return send(
-            code.at[p, v], land.at[p, v], send_sem.at[0], recv_sem.at[p % GROUPS], routes[p]["ways"][v][to]
+            code.at[p, v], land.at[p, v], send_sem.at[0], recv_sem.at[p], routes[p]["ways"][v][to]
         )
 
     def arrived(block, recv_sem, slot):
@@ -530,7 +530,7 @@
         second = routes[p]["second"]
         return [
             send(
-                code3.at[p, k], land3.at[p, k], send3.at[0], recv3.at[p % GROUPS],
+                code3.at[p, k], land3.at[p, k], send3.at[0], recv3.at[p],
                 chip(**{second: other}),
             )
             for k, other in enumerate(ring_peers(second, RING))
@@ -629,16 +629,14 @@
     small_start(1)
     order = [h * GROUPS + g for g in range(GROUPS) for h in range(2)]
     for p in order:
-        if p < GROUPS:
-            arrived(land1.at[pl.ds(0, 2)], recv1, p)
+        arrived(land1.at[p], recv1, p)
         for v, way in enumerate(routes[p]["ways"]):
             absorb(p, way["four"], 4, [(land1, (p, v))])
         start2(p)
     small_end(1)
     small_start(2)
     for p in order:
-        if p < GROUPS:
-            arrived(land2.at[pl.ds(0, 2)], recv2, p)
+        arrived(land2.at[p], recv2, p)
         for v, way in enumerate(routes[p]["ways"]):
             absorb(p, way["two"], 2, [(land2, (p, v))])
         start3(p)
@@ -651,8 +649,7 @@
         return send(code4.at[p], land4.at[z], send4.at[0], recv4.at[0], chip(z=p))
 
     for p in order:
-        if p < GROUPS:
-            arrived(land3.at[pl.ds(0, 2)], recv3, p)
+        arrived(land3.at[p], recv3, p)
         absorb(p, routes[p]["unit"], 1, [(land3, (p, k)) for k in range(RING - 1)])
 
         @pl.when(z != p)
@@ -686,17 +683,17 @@
         second = routes[p]["second"]
         block = full.at[p, core, routes[p]["unit"]]
         return [
-            send(block, block, qsend.at[0], qrecv.at[p % GROUPS], chip(**{second: other}))
+            send(block, block, qsend.at[0], qrecv.at[p], chip(**{second: other}))
             for k, other in enumerate(ring_peers(second, RING))
         ]
 
     def far_copy(p, v):
         block = full.at[p, core, pl.ds(routes[p]["ways"][v]["two"], 2)]
-        return send(block, block, far_send.at[0], far_recv.at[p % GROUPS], routes[p]["ways"][v]["far"])
+        return send(block, block, far_send.at[0], far_recv.at[p], routes[p]["ways"][v]["far"])
 
     def near_copy(p, v):
         block = full.at[p, core, pl.ds(routes[p]["ways"][v]["four"], 4)]
-        return send(block, block, near_send.at[0], near_recv.at[p % GROUPS], routes[p]["ways"][v]["near"])
+        return send(block, block, near_send.at[0], near_recv.at[p], routes[p]["ways"][v]["near"])
 
     def core_start(p, second):
         for way in routes[p]["ways"]:
@@ -714,8 +711,7 @@
         for copy in qcopies(p):
             copy.start()
     for p in order:
-        if p < GROUPS:
-            arrived(units(2 * (RING - 1)), qrecv, p)
+        arrived(units(RING - 1), qrecv, p)
         for v in range(WAYS):
             far_copy(p, v).start()
     def reveal(p, c, which):
@@ -744,8 +740,7 @@
         reveal(p, 1 - core, "other4" if second else "four")
 
     for k, p in enumerate(order):
-        if p < GROUPS:
-            arrived(units(8), far_recv, p)
+        arrived(units(4), far_recv, p)
         for v in range(WAYS):
             near_copy(p, v).start()
         core_start(p, 0)
@@ -754,8 +749,7 @@
     reveal(order[-1], core, "four")
     for k, p in enumerate(order):
         reveal_core(p, 0)
-        if p < GROUPS:
-            arrived(units(16), near_recv, p)
+        arrived(units(8), near_recv, p)
         core_start(p, 1)
         if k >= 1:
             reveal(order[k - 1], core, "other4")
@@ -844,8 +838,8 @@
             pltpu.VMEM((5 * SUB, LANES), jnp.float32),
             pltpu.VMEM((smalls * SUB, LANES), jnp.float32),
             dma((4,)), *both(6), *both(16), *both(2), *both(4),
-            *one(GROUPS), *one(GROUPS), *one(GROUPS), *one(1),
-            *one(DEEP), *one(GROUPS), *one(GROUPS), *one(GROUPS), *one(2 * GROUPS), *one(4),
+            *one(PARTS), *one(PARTS), *one(PARTS), *one(1),
+            *one(DEEP), *one(PARTS), *one(PARTS), *one(PARTS), *one(2 * GROUPS), *one(4),
         ],
         compiler_params=pltpu.CompilerParams(
             collective_id=0, has_side_effects=True, vmem_limit_bytes=40 * 1024 * 1024

time: 74.9 us -> 74.6 us (level)
  no operation moved by 1% of the time
where the time goes in v8:
time: 74.6 us; the launch traced here: 74.5 us
  Pallas kernels  73.9 us (99%)
    pallas_call x1, Pallas kernels, per_device(): pl.pallas_call(functools.partial(kernel, sizes), out_shape=(jax.ShapeDtyp...  70.9 us
    pallas_call x1, Pallas kernels, per_device(): pl.pallas_call(store_kernel, out_shape=(jax.ShapeDtypeStruct((TAPS ** 3,...  3.01 us

profile of v8, /device:TPU:1, one launch (start us, length us, event | category | flops | bytes accessed | tf_op | source)
XLA Modules:
  0.0 74.5 jit_solution(3795663304288343283)
XLA Ops:
  0.6 70.9 %shard_map.67 = (f32[27,32,8,256]{3,2,1,0:T(8,128)S(1)}, f32[1,256]{1,0:T(1,128)S(1)}, f32[1,256]{1,0:T(1,128)S(1)}) custom-call(bf16[2,128,256]{2,1,0:T(8,128)(2,1)} %bitcast.8, bf16[27,256,256]{2,1,0:T(8,128)(2,1)} %bitcast.7, f32[1,256]{1,0:T(1,128)} %bitcast.9, f32[1,256]{1,0:T(1,128)} %bitcast.10), custom_call_target="tpu_custom_call" | custom-call | tf_op jit(solution)/shard_map/pallas_call | solution.py:809
  71.5 3.0 %shard_map.68 = (f32[27,32,8,256]{3,2,1,0:T(8,128)}, f32[1,256]{1,0:T(1,128)}, f32[1,256]{1,0:T(1,128)}) custom-call(f32[27,32,8,256]{3,2,1,0:T(8,128)S(1)} %get-tuple-element.9.grad_ref, f32[1,256]{1,0:T(1,128)S(1)} %get-tuple-element.10.bias_ref, f32[1,256]{1,0:T(1,128)S(1)} %get-tuple-element.11.head_ref), custom_call_target="tpu_custom_call" | custom-call | tf_op jit(solution)/shard_map/pallas_call | solution.py:856

commit v9 on v8

--- a/solution.py
+++ b/solution.py
@@ -768,15 +768,15 @@
 
 
 def store_kernel(grad_ref, bias_ref, head_ref, grad_out, bias_out, head_out, sem):
-    step = TAPS
+    step = TAPS**2
     copies = [
         pltpu.make_async_copy(
             grad_ref.at[pl.ds(k * step, step)], grad_out.at[pl.ds(k * step, step)], sem.at[k]
         )
         for k in range(TAPS**3 // step)
     ]
-    copies.append(pltpu.make_async_copy(bias_ref, bias_out, sem.at[TAPS**2]))
-    copies.append(pltpu.make_async_copy(head_ref, head_out, sem.at[TAPS**2 + 1]))
+    copies.append(pltpu.make_async_copy(bias_ref, bias_out, sem.at[TAPS]))
+    copies.append(pltpu.make_async_copy(head_ref, head_out, sem.at[TAPS + 1]))
     for copy in copies:
         copy.start()
     for copy in copies:
@@ -860,7 +860,7 @@
         ),
         in_specs=[vmem, vmem, vmem],
         out_specs=(hbm, hbm, hbm),
-        scratch_shapes=[dma((TAPS**2 + 2,))],
+        scratch_shapes=[dma((TAPS + 2,))],
         compiler_params=pltpu.CompilerParams(vmem_limit_bytes=8 * 1024 * 1024),
     )(grad_weight, grad_bias, grad_head)
     grad_weight = grad_weight.reshape(TAPS, TAPS, TAPS, chans, chans)

time: 74.6 us -> 74.6 us (level)
  no operation moved by 1% of the time
where the time goes in v9:
time: 74.6 us; the launch traced here: 74.5 us
  Pallas kernels  73.9 us (99%)
    pallas_call x1, Pallas kernels, per_device(): pl.pallas_call(functools.partial(kernel, sizes), out_shape=(jax.ShapeDtyp...  70.9 us
    pallas_call x1, Pallas kernels, per_device(): pl.pallas_call(store_kernel, out_shape=(jax.ShapeDtypeStruct((TAPS ** 3,...  3.01 us

profile of v9, /device:TPU:1, one launch (start us, length us, event | category | flops | bytes accessed | tf_op | source)
XLA Modules:
  0.0 74.5 jit_solution(12740857934951187096)
XLA Ops:
  0.6 70.9 %shard_map.67 = (f32[27,32,8,256]{3,2,1,0:T(8,128)S(1)}, f32[1,256]{1,0:T(1,128)S(1)}, f32[1,256]{1,0:T(1,128)S(1)}) custom-call(bf16[2,128,256]{2,1,0:T(8,128)(2,1)} %bitcast.8, bf16[27,256,256]{2,1,0:T(8,128)(2,1)} %bitcast.7, f32[1,256]{1,0:T(1,128)} %bitcast.9, f32[1,256]{1,0:T(1,128)} %bitcast.10), custom_call_target="tpu_custom_call" | custom-call | tf_op jit(solution)/shard_map/pallas_call | solution.py:809
  71.5 3.0 %shard_map.68 = (f32[27,32,8,256]{3,2,1,0:T(8,128)}, f32[1,256]{1,0:T(1,128)}, f32[1,256]{1,0:T(1,128)}) custom-call(f32[27,32,8,256]{3,2,1,0:T(8,128)S(1)} %get-tuple-element.9.grad_ref, f32[1,256]{1,0:T(1,128)S(1)} %get-tuple-element.10.bias_ref, f32[1,256]{1,0:T(1,128)S(1)} %get-tuple-element.11.head_ref), custom_call_target="tpu_custom_call" | custom-call | tf_op jit(solution)/shard_map/pallas_call | solution.py:856
